TPU v7x, 8 devices: a whole 2x2x1 slice. The times are simulated.
8 devices in a mesh: dp: 1 (over z), tp: 8 (over x, y, core).
Axes of the slice: x: 2, y: 2, z: 1, core: 2. Of those that a mesh axis runs over, the one named last changes fastest.
Arguments:
- x: bfloat16 [4096, 2048], P(('dp', 'tp'))
- dy: bfloat16 [4096, 2048], P(('dp', 'tp'))
- gate: bfloat16 [4096, 5120], P('dp', 'tp')
- up: bfloat16 [4096, 5120], P('dp', 'tp')
- w_gate: bfloat16 [2048, 5120], P(None, 'tp')
- w_up: bfloat16 [2048, 5120], P(None, 'tp')
- w_down: bfloat16 [5120, 2048], P('tp')
Outputs:
- output 1: bfloat16 [4096, 2048], P(('dp', 'tp'))
- output 2: bfloat16 [2048, 5120], P('dp', 'tp')
- output 3: bfloat16 [2048, 5120], P('dp', 'tp')
- output 4: bfloat16 [5120, 2048], P(('dp', 'tp'))
All inputs are finite; a program needn't handle non-finite values.
Results may differ from a plain program's by a relative error of at most 0.012.
Values are sent between devices in bfloat16 or wider.
A program may use at most 2 GiB of HBM per device.

v0:
```python
import jax
import jax.numpy as jnp


def act(gate, up):
    return jax.nn.gelu(gate) * up


def solution(mesh):
    def step(x, dy, gate, up, w_gate, w_up, w_down):
        hidden, back = jax.vjp(act, gate.astype(jnp.float32), up.astype(jnp.float32))
        d_hidden = jnp.dot(dy, w_down.T, preferred_element_type=jnp.float32)
        d_gate, d_up = (g.astype(jnp.bfloat16) for g in back(d_hidden))
        dx = jnp.dot(d_gate, w_gate.T) + jnp.dot(d_up, w_up.T)
        groups = mesh.shape["dp"]

        def by_group(a, b):
            a, b = (t.reshape(groups, -1, t.shape[-1]) for t in (a, b))
            product = jnp.einsum("gta,gtb->gab", a, b, preferred_element_type=jnp.float32)
            return product.astype(jnp.bfloat16).reshape(-1, b.shape[-1])

        return dx, by_group(x, d_gate), by_group(x, d_up), by_group(hidden.astype(jnp.bfloat16), dy)

    return step
```

profile of v0, /device:TPU:1, one launch (start us, length us, event | category | flops | bytes accessed | tf_op | source)
XLA Modules:
  0.0 299.0 jit_solution(3235450216724664854)
XLA Ops:
  7.2 0.0 copy-start
  7.2 0.0 all-gather.7.cloned.1.call-start
  7.2 0.7 all-gather.7.cloned.1.call-update
  7.9 0.0 all-gather.9.cloned.1.call-start
  8.0 0.7 all-gather.9.cloned.1.call-update
  8.7 0.0 reduce-scatter.4.cloned.1.call-start
  8.7 87.4 %all-gather.7.cloned.1.call-done = bf16[4096,2048]{1,0:T(8,128)(2,1)} async-done(((bf16[512,2048]{1,0:T(8,128)(2,1)}), bf16[4096,2048]{1,0:T(8,128)(2,1)}) %all-gather.7.cloned.1.call-update) | async-done | bytes 16777232 | tf_op args[1]
  96.1 29.2 %fusion.4 = (bf16[4096,640]{1,0:T(8,128)(2,1)}, f32[4096,640]{1,0:T(8,128)}) fusion(bf16[4096,640]{1,0:T(8,128)(2,1)} %param.3, bf16[4096,640]{1,0:T(8,128)(2,1)} %param.2, bf16[4096,2048]{1,0:T(8,128)(2,1)} %all-gather.7.cloned.1.call-done, bf16[640,2048]{1,0:T(8,128)(2,1)} %param.1), kind=kOutput, calls=%fused_computation.12 | convolution fusion | flops 10797711360 | bytes 45613056 | tf_op jit(solution)/dot_general | solution.py:12
  125.4 0.0 copy-done
  125.4 18.7 %fusion.25 = bf16[4096,2048]{1,0:T(8,128)(2,1)} fusion(bf16[4096,640]{1,0:T(8,128)(2,1)} %get-tuple-element.4, bf16[2048,640]{1,0:T(8,128)(2,1)S(1)} %copy-done), kind=kOutput, calls=%fused_computation.33 | convolution fusion | flops 10737418240 | bytes 24641536 | tf_op jit(solution)/dot_general | solution.py:14
  144.0 23.9 %convolution_add_fusion = bf16[4096,2048]{1,0:T(8,128)(2,1)} fusion(bf16[4096,2048]{1,0:T(8,128)(2,1)} %fusion.25, bf16[2048,640]{1,0:T(8,128)(2,1)} %param.5, f32[4096,640]{1,0:T(8,128)} %get-tuple-element.5, bf16[4096,640]{1,0:T(8,128)(2,1)} %param.3), kind=kOutput, calls=%fused_computation.8 | convolution fusion | flops 10774642688 | bytes 51904512 | tf_op jit(solution)/dot_general | solution.py:14
  167.9 0.0 reduce-scatter.4.cloned.1.call-update
  167.9 14.1 %all-gather.9.cloned.1.call-done = bf16[4096,2048]{1,0:T(8,128)(2,1)} async-done(((bf16[512,2048]{1,0:T(8,128)(2,1)}), bf16[4096,2048]{1,0:T(8,128)(2,1)}) %all-gather.9.cloned.1.call-update) | async-done | bytes 16777232 | tf_op args[0]
  182.1 21.5 %fusion.20 = bf16[2048,640]{0,1:T(8,128)(2,1)S(1)} fusion(bf16[4096,2048]{1,0:T(8,128)(2,1)} %all-gather.9.cloned.1.call-done, f32[4096,640]{1,0:T(8,128)} %get-tuple-element.5, bf16[4096,640]{1,0:T(8,128)(2,1)} %param.3), kind=kOutput, calls=%fused_computation.28 | convolution fusion | flops 10767564800 | bytes 35127296 | tf_op jit(solution)/gta,gtb->gab/dot_general | solution.py:19
  203.6 2.6 copy.1
  206.1 16.2 %fusion.19 = bf16[2048,640]{0,1:T(8,128)(2,1)S(1)} fusion(bf16[4096,640]{1,0:T(8,128)(2,1)} %get-tuple-element.4, bf16[4096,2048]{1,0:T(8,128)(2,1)} %all-gather.9.cloned.1.call-done), kind=kOutput, calls=%fused_computation.27 | convolution fusion | flops 10738728960 | bytes 24641536 | tf_op jit(solution)/gta,gtb->gab/dot_general | solution.py:19
  222.3 2.6 copy
  224.9 0.0 copy-start.1
  224.9 22.1 %fusion.16 = bf16[640,2048]{1,0:T(8,128)(2,1)} fusion(bf16[4096,2048]{1,0:T(8,128)(2,1)} %all-gather.7.cloned.1.call-done, bf16[4096,640]{1,0:T(8,128)(2,1)} %param.2, bf16[4096,640]{1,0:T(8,128)(2,1)} %param.3), kind=kOutput, calls=%fused_computation.24 | convolution fusion | flops 10770186240 | bytes 29884416 | tf_op jit(solution)/gta,gtb->gab/dot_general | solution.py:19
  247.0 45.4 %reduce-scatter.4.cloned.1.call-done = bf16[512,2048]{1,0:T(8,128)(2,1)} async-done(((bf16[4096,2048]{1,0:T(8,128)(2,1)}), bf16[512,2048]{1,0:T(8,128)(2,1)}) %reduce-scatter.4.cloned.1.call-update) | async-done | bytes 2097168
  292.4 0.0 copy-done.1
Async XLA Ops:
  7.2 118.2 %copy-start = (bf16[2048,640]{1,0:T(8,128)(2,1)S(1)}, bf16[2048,640]{1,0:T(8,128)(2,1)}, u32[]{:S(2)}) copy-start(bf16[2048,640]{1,0:T(8,128)(2,1)} %param.4) | copy-start | bytes 7864324
  7.2 89.0 %all-gather.7.cloned.1.call-start = ((), (), s32[]{:S(2)}) async-start(), calls=%async_computation.1 | async-start | bytes 18874368 | tf_op args[1]
  7.9 174.1 %all-gather.9.cloned.1.call-start = ((), (), s32[]{:S(2)}) async-start(), calls=%async_computation.2 | async-start | bytes 18874368 | tf_op args[0]
  8.7 283.8 %reduce-scatter.4.cloned.1.call-start = ((), (), s32[]{:S(2)}) async-start(), calls=%async_computation.3 | async-start | bytes 18874368
  224.9 67.5 %copy-start.1 = (bf16[2048,640]{1,0:T(8,128)(2,1)S(1)}, bf16[2048,640]{1,0:T(8,128)(2,1)}, u32[]{:S(2)}) copy-start(bf16[2048,640]{1,0:T(8,128)(2,1)} %param.4) | copy-start | bytes 7864324
Sparse Core Ops, SparseCore 0:
  9.8 86.2 all-gather.6
  98.0 84.0 all-gather.8
  186.1 106.2 reduce-scatter.3
where the time goes:
time: 300 us; the launch traced here: 299 us
  waiting for transfers between devices  148 us (49%)
  matrix products  132 us (44%)
  between operations  13.8 us (5%)
  local copies, waits for them, and re-layouts  5.16 us (2%)
    unnamed x6, waiting for transfers between devices  148 us
    dot_general x3, matrix products, by_group(): jnp.einsum('gta,gtb->gab', a, b, preferred_element_type=jnp.float32)  59.8 us
    dot_general x2, matrix products, step(): dx = jnp.dot(d_gate, w_gate.T) + jnp.dot(d_up, w_up.T)  42.5 us
    dot_general x1, matrix products, step(): d_hidden = jnp.dot(dy, w_down.T, preferred_element_type=jnp.float32)  29.2 us
  transfers between devices with their start and end apart: 3, of which 3 were waited for; matrix products, arithmetic and copies ran while one was open for 46% of the time, Pallas kernels for 0%

commit v1 on v0

v1 whole, which is shorter than its diff:
```python
import functools

import jax
import jax.numpy as jnp
from jax import lax
from jax.experimental import pallas as pl
from jax.experimental.pallas import tpu as pltpu
from jax.sharding import PartitionSpec as P

D = 2048
F = 640
B = 512
H = 256
F32 = jnp.float32
BF16 = jnp.bfloat16
NT = (((1,), (1,)), ((), ()))
TN = (((0,), (0,)), ((), ()))
C0 = 0.7978845608028654
C1 = 0.7978845608028654 * 0.044715


def kernel(
    x_ref, dy_ref, gate_ref, up_ref, wg_ref, wu_ref, wd_ref,
    dx_ref, dwg_ref, dwu_ref, dwd_ref, dy_all, x_all, rs_in,
    wd, wgu, dgu, dwd_acc, dwgu_acc, own, tok, gv, uv, dh, hid, p_in, p_out, rs_out,
    dy_ss, dy_rs, dyp_ss, dyp_rs, x_ss, x_rs, xp_ss, xp_rs, p_ss, p_rs, r_ss, r_rs, w_sem, t_sem, g_sem, o_sem,
):
    me = lax.axis_index("tp")
    core, iy, ix = me % 2, (me // 2) % 2, me // 4
    other = 1 - 2 * core
    partner = me + other
    ny = me + 2 - 4 * iy
    nx = me + 4 - 8 * ix
    nd = ny + 4 - 8 * ix

    barrier = pltpu.get_barrier_semaphore()
    for d in (partner, nx, ny):
        pl.semaphore_signal(barrier, inc=1, device_id={"tp": d}, device_id_type=pl.DeviceIdType.MESH)
    pl.semaphore_wait(barrier, 3)

    def owner(g):
        return jnp.where(g < 2, me, jnp.where(g >= 6, nd, jnp.where(g % 2 == 0, nx, ny)))

    def half(g):
        return jnp.where(g == 4, 1, jnp.where(g == 5, 0, g % 2))

    def rows(dev, h):
        return pl.ds(pl.multiple_of(dev * B + h * H, H), H)

    def remote(src, dst, ss, rs, dev):
        return pltpu.make_async_remote_copy(
            src_ref=src, dst_ref=dst, send_sem=ss, recv_sem=rs, device_id={"tp": dev}, device_id_type=pl.DeviceIdType.MESH
        )

    def send_own(ref, full, ss, rs, h, g, dev):
        return remote(ref.at[pl.ds(h * H, H)], full.at[rows(me, h)], ss.at[g], rs.at[g], dev)

    def send_on(full, ss, rs, g_in, g_out, dev):
        r = rows(owner(g_in), half(g_in))
        return remote(full.at[r], full.at[r], ss.at[g_out], rs.at[g_out], dev)

    def start_own(ref, full, ss, rs, pss, prs):
        send_own(ref, full, ss, rs, 0, 2, nx).start()
        send_own(ref, full, ss, rs, 1, 3, ny).start()
        send_own(ref, full, pss, prs, 0, 0, partner).start()
        send_own(ref, full, ss, rs, 1, 4, nx).start()
        send_own(ref, full, ss, rs, 0, 5, ny).start()
        send_own(ref, full, pss, prs, 1, 1, partner).start()

    def arrived(full, ss, rs, g):
        send_on(full, ss, rs, g, g, partner).wait_recv()

    def relay(full, ss, rs, pss, prs, g, onward):
        arrived(full, ss, rs, g)
        if onward == "y":
            send_on(full, ss, rs, g, 6, ny).start()
        if onward == "x":
            send_on(full, ss, rs, g, 7, nx).start()
        send_on(full, pss, prs, g, g, partner).start()

    def load_tokens(ref, full, g):
        o, h = owner(g), half(g)
        p = pltpu.make_async_copy(full.at[rows(o + other, h)], tok.at[pl.ds(0, H)], t_sem.at[0])
        p.start()

        @pl.when(g < 2)
        def _():
            pltpu.make_async_copy(ref.at[pl.ds(pl.multiple_of(h * H, H), H)], tok.at[pl.ds(H, H)], t_sem.at[1]).start()

        @pl.when(g >= 2)
        def _():
            pltpu.make_async_copy(full.at[rows(o, h)], tok.at[pl.ds(H, H)], t_sem.at[1]).start()

        p.wait()
        pltpu.make_async_copy(full.at[rows(o, h)], tok.at[pl.ds(H, H)], t_sem.at[1]).wait()

    def gate_copies(g):
        o, h = owner(g), half(g)
        for i, (src, dst) in enumerate(((gate_ref, gv), (up_ref, uv))):
            yield pltpu.make_async_copy(src.at[rows(o + other, h)], dst.at[pl.ds(0, H)], g_sem.at[2 * i])
            yield pltpu.make_async_copy(src.at[rows(o, h)], dst.at[pl.ds(H, H)], g_sem.at[2 * i + 1])

    start_own(dy_ref, dy_all, dy_ss, dy_rs, dyp_ss, dyp_rs)
    weights = (
        pltpu.make_async_copy(wd_ref, wd, w_sem.at[0]),
        pltpu.make_async_copy(wg_ref, wgu.at[:, pl.ds(0, F)], w_sem.at[1]),
        pltpu.make_async_copy(wu_ref, wgu.at[:, pl.ds(F, F)], w_sem.at[2]),
    )
    for w in weights:
        w.start()
    for c in gate_copies(0):
        c.start()
    dwd_acc[...] = jnp.zeros_like(dwd_acc)
    dwgu_acc[...] = jnp.zeros_like(dwgu_acc)
    for w in weights:
        w.wait()

    def send_p(g):
        return remote(p_out.at[g % 2], p_in.at[g], p_ss.at[g], p_rs.at[g], partner)

    def send_r(stage, slot, dev):
        return remote(rs_out.at[stage], rs_in.at[slot], r_ss.at[slot], r_rs.at[slot], dev)

    def dx_tile(g, r0, j):
        a = dgu[pl.ds(pl.multiple_of(g * B + r0, H), H), :]
        w = wgu[pl.ds(pl.multiple_of(j * 512, 512), 512), :]
        return lax.dot_general(a, w, NT, preferred_element_type=F32)

    def first_pass(g, carry):
        @pl.when(g == 2)
        def _():
            relay(dy_all, dy_ss, dy_rs, dyp_ss, dyp_rs, 2, "y")
            relay(dy_all, dy_ss, dy_rs, dyp_ss, dyp_rs, 3, "x")
            start_own(x_ref, x_all, x_ss, x_rs, xp_ss, xp_rs)

        for k in (4, 6):
            @pl.when(g == k)
            def _():
                relay(dy_all, dy_ss, dy_rs, dyp_ss, dyp_rs, k, None)
                relay(dy_all, dy_ss, dy_rs, dyp_ss, dyp_rs, k + 1, None)

        arrived(dy_all, dyp_ss, dyp_rs, g)
        load_tokens(dy_ref, dy_all, g)
        for c in gate_copies(g):
            c.wait()

        for n0, n in ((0, 256), (256, 256), (512, 128)):
            dh[:, n0:n0 + n] = lax.dot_general(tok[...], wd[n0:n0 + n, :], NT, preferred_element_type=F32)

        def gates(i, carry):
            r = pl.ds(pl.multiple_of(i * 32, 32), 32)
            a, u, d = gv[r, :].astype(F32), uv[r, :].astype(F32), dh[r, :]
            a2 = a * a
            t = jnp.tanh(a * (C0 + C1 * a2))
            cdf = 0.5 + 0.5 * t
            gelu = a * cdf
            slope = cdf + (0.5 * a) * ((1.0 - t * t) * (C0 + (3.0 * C1) * a2))
            hid[r, :] = (gelu * u).astype(BF16)
            q = pl.ds(pl.multiple_of(g * B + i * 32, 32), 32)
            dgu[q, 0:F] = (d * u * slope).astype(BF16)
            dgu[q, F:2 * F] = (d * gelu).astype(BF16)
            return carry

        lax.fori_loop(0, B // 32, gates, 0)

        @pl.when(g < 7)
        def _():
            for c in gate_copies(g + 1):
                c.start()

        @pl.when(g >= 2)
        def _():
            send_p(g - 2).wait_send()

        def p_rows(j, carry):
            p_out[g % 2, :, pl.ds(pl.multiple_of(j * 512, 512), 512)] = dx_tile(g, 0, j).astype(BF16)
            return carry

        lax.fori_loop(0, 4, p_rows, 0)
        send_p(g).start()

        def down(j, carry):
            s = pl.ds(pl.multiple_of(j * 512, 512), 512)
            dwd_acc[:, s] += lax.dot_general(hid[...], tok[:, s], TN, preferred_element_type=F32)
            return carry

        lax.fori_loop(0, 4, down, 0)

        send_p(g).wait_recv()

        @pl.when(jnp.logical_or(g < 4, g >= 6))
        def _():
            stage = jnp.where(g >= 6, g - 4, g % 2)

            def m_rows(j, carry):
                s = pl.ds(pl.multiple_of(j * 512, 512), 512)
                total = dx_tile(g, H, j) + p_in[g, :, s].astype(F32)

                @pl.when(g < 2)
                def _():
                    own[pl.ds(pl.multiple_of((g % 2) * H, H), H), s] = total

                @pl.when(g >= 2)
                def _():
                    rs_out[stage, :, s] = total.astype(BF16)

                return carry

            lax.fori_loop(0, 4, m_rows, 0)

        @pl.when(g == 2)
        def _():
            send_r(0, 2, nx).start()

        @pl.when(g == 3)
        def _():
            send_r(1, 3, ny).start()

        @pl.when(g == 6)
        def _():
            send_r(2, 0, nx).start()

        @pl.when(g == 7)
        def _():
            send_r(3, 1, ny).start()

        return carry

    lax.fori_loop(0, 8, first_pass, 0)

    def down_out(k, carry):
        for i in range(5):
            p_in[i // 2, (i % 2) * 128:(i % 2) * 128 + 128, pl.ds(pl.multiple_of(k * 256, 256), 256)] = dwd_acc[
                i * 128:i * 128 + 128, pl.ds(pl.multiple_of(k * 256, 256), 256)
            ].astype(BF16)
        return carry

    lax.fori_loop(0, 8, down_out, 0)
    down_copies = [
        pltpu.make_async_copy(p_in.at[i, pl.ds(0, n)], dwd_ref.at[pl.ds(i * H, n)], o_sem.at[i])
        for i, n in enumerate((H, H, 128))
    ]
    for c in down_copies:
        c.start()

    relay(x_all, x_ss, x_rs, xp_ss, xp_rs, 2, "y")
    relay(x_all, x_ss, x_rs, xp_ss, xp_rs, 3, "x")

    def fetch(slot, k):
        c = pltpu.make_async_copy(rs_in.at[slot], tok.at[pl.ds(k * H, H)], t_sem.at[k])
        c.start()
        return c

    def add_own(pairs):
        for slot, h in pairs:
            send_r(0, slot, nx).wait_recv()
            fetch(slot, h).wait()

    def second_pass(g, carry):
        @pl.when(g == 4)
        def _():
            relay(x_all, x_ss, x_rs, xp_ss, xp_rs, 4, None)
            relay(x_all, x_ss, x_rs, xp_ss, xp_rs, 5, None)

        @pl.when(g == 6)
        def _():
            add_own(((2, 0), (3, 1)))

            def add(i, carry):
                r = pl.ds(pl.multiple_of(i * 32, 32), 32)
                own[r, :] += tok[r, :].astype(F32)
                return carry

            lax.fori_loop(0, B // 32, add, 0)

            send_r(0, 2, nx).wait_send()
            send_r(1, 3, ny).wait_send()
            for group, slot, k in ((4, 1, 0), (5, 0, 1)):
                send_r(0, slot, nx).wait_recv()
                fetch(slot, k).wait()

                def late(j, carry):
                    s = pl.ds(pl.multiple_of(j * 512, 512), 512)
                    total = dx_tile(group, H, j) + p_in[group, :, s].astype(F32) + tok[k * H:(k + 1) * H, s].astype(F32)
                    rs_out[k, :, s] = total.astype(BF16)
                    return carry

                lax.fori_loop(0, 4, late, 0)
                send_r(k, 4 + k, (nx, ny)[k]).start()

            relay(x_all, x_ss, x_rs, xp_ss, xp_rs, 6, None)
            relay(x_all, x_ss, x_rs, xp_ss, xp_rs, 7, None)

        arrived(x_all, xp_ss, xp_rs, g)
        load_tokens(x_ref, x_all, g)

        def weight(j, carry):
            s = pl.ds(pl.multiple_of(j * 512, 512), 512)
            d = dgu[pl.ds(pl.multiple_of(g * B, B), B), :]
            dwgu_acc[s, :] += lax.dot_general(tok[:, s], d, TN, preferred_element_type=F32)
            return carry

        lax.fori_loop(0, 4, weight, 0)
        return carry

    lax.fori_loop(0, 8, second_pass, 0)

    def weight_out(i, carry):
        r = pl.ds(pl.multiple_of(i * 32, 32), 32)
        dgu[r, :] = dwgu_acc[r, :].astype(BF16)
        return carry

    lax.fori_loop(0, D // 32, weight_out, 0)
    weight_copies = (
        pltpu.make_async_copy(dgu.at[pl.ds(0, D), pl.ds(0, F)], dwg_ref, o_sem.at[3]),
        pltpu.make_async_copy(dgu.at[pl.ds(0, D), pl.ds(F, F)], dwu_ref, o_sem.at[4]),
    )
    for c in weight_copies:
        c.start()

    add_own(((5, 0), (4, 1)))

    def finish(i, carry):
        r = pl.ds(pl.multiple_of(i * 32, 32), 32)
        tok[r, :] = (own[r, :] + tok[r, :].astype(F32)).astype(BF16)
        return carry

    lax.fori_loop(0, B // 32, finish, 0)
    out = pltpu.make_async_copy(tok, dx_ref, o_sem.at[5])
    out.start()

    for c in down_copies + list(weight_copies) + [out]:
        c.wait()
    for full, ss, rs, pss, prs in ((dy_all, dy_ss, dy_rs, dyp_ss, dyp_rs), (x_all, x_ss, x_rs, xp_ss, xp_rs)):
        for g in range(8):
            send_on(full, pss, prs, g, g, partner).wait_send()
            if g >= 2:
                send_on(full, ss, rs, g, g, partner).wait_send()
    for g in (6, 7):
        send_p(g).wait_send()
    for stage, slot in ((2, 0), (3, 1), (0, 4), (1, 5)):
        send_r(stage, slot, nx).wait_send()


def solution(mesh):
    def local(*args):
        any_ = pl.BlockSpec(memory_space=pl.ANY)
        dma = pltpu.SemaphoreType.DMA
        shapes = [(B, D), (D, F), (D, F), (F, D), (8 * B, D), (8 * B, D), (6, H, D)]
        outs = pl.pallas_call(
            kernel,
            out_shape=[jax.ShapeDtypeStruct(s, BF16) for s in shapes],
            in_specs=[any_] * 7,
            out_specs=[any_] * 7,
            scratch_shapes=[
                pltpu.VMEM((F, D), BF16),
                pltpu.VMEM((D, 2 * F), BF16),
                pltpu.VMEM((8 * B, 2 * F), BF16),
                pltpu.VMEM((F, D), F32),
                pltpu.VMEM((D, 2 * F), F32),
                pltpu.VMEM((B, D), F32),
                pltpu.VMEM((B, D), BF16),
                pltpu.VMEM((B, F), BF16),
                pltpu.VMEM((B, F), BF16),
                pltpu.VMEM((B, F), F32),
                pltpu.VMEM((B, F), BF16),
                pltpu.VMEM((8, H, D), BF16),
                pltpu.VMEM((2, H, D), BF16),
                pltpu.VMEM((4, H, D), BF16),
            ]
            + [dma((8,))] * 12
            + [dma((3,)), dma((2,)), dma((4,)), dma((6,))],
            compiler_params=pltpu.CompilerParams(collective_id=0, has_side_effects=True, vmem_limit_bytes=67043328),
            name="backward",
        )(*args)
        return tuple(outs[:4])

    rows, cols = P(("dp", "tp"), None), P("dp", "tp")
    return jax.shard_map(
        local,
        mesh=mesh,
        in_specs=(rows, rows, cols, cols, P(None, "tp"), P(None, "tp"), P("tp", None)),
        out_specs=(rows, cols, cols, rows),
        check_vma=False,
    )
```

time: 300 us -> 224 us (0.75)
  Pallas kernels: 0 us -> 211 us
  waiting for transfers between devices: 148 us -> 0 us
  matrix products: 132 us -> 0 us
  between operations: 13.8 us -> 0.65 us
  local copies, waits for them, and re-layouts: 5.16 us -> 10.2 us
    pallas_call x0 -> x1, Pallas kernels: none -> 211 us  [local(): pl.pallas_call(kernel, out_shape=[jax.ShapeDtypeStruct(s, BF16) for s in...]
    unnamed x6 -> x0, waiting for transfers between devices: 148 us -> none
    dot_general x6 -> x0, matrix products: 132 us -> none  [the longest x3 59.8 us: by_group(): jnp.einsum('gta,gtb->gab', a, b, preferred_element_type=jnp.float32)]
    unnamed x6 -> x10, local copies, waits for them, and re-layouts: 5.16 us -> 10.2 us
  transfers between devices with their start and end apart: 3 -> 0, of which waited for: 3 -> 0; matrix products, arithmetic and copies ran while one was open for 46% -> 0% of each run, Pallas kernels for 0% -> 0%
where the time goes in v1:
time: 224 us; the launch traced here: 222 us
  Pallas kernels  211 us (94%)
  local copies, waits for them, and re-layouts  10.2 us (5%)
    pallas_call x1, Pallas kernels, local(): pl.pallas_call(kernel, out_shape=[jax.ShapeDtypeStruct(s, BF16) for s in...  211 us
    unnamed x10, local copies, waits for them, and re-layouts  10.2 us

profile of v1, /device:TPU:1, one launch (start us, length us, event | category | flops | bytes accessed | tf_op | source)
XLA Modules:
  0.0 221.8 jit_solution(3806064272593197902)
XLA Ops:
  0.6 211.0 %backward.1 = (bf16[512,2048]{1,0:T(8,128)(2,1)}, bf16[2048,640]{1,0:T(8,128)(2,1)}, bf16[2048,640]{1,0:T(8,128)(2,1)}, bf16[640,2048]{1,0:T(8,128)(2,1)}, bf16[...) custom-call(bf16[512,2048]{1,0:T(8,128)(2,1)} %x_ref.1, ...), custom_call_target="tpu_custom_call" | custom-call | tf_op jit(solution)/shard_map/backward/pallas_call | solution.py:350
  211.6 0.0 copy-start.2
  211.6 3.3 %copy.15 = bf16[512,2048]{1,0:T(8,128)(2,1)} copy(bf16[512,2048]{1,0:T(8,128)(2,1)} %get-tuple-element.16) | data formatting | bytes 4194304
  214.9 0.0 copy-done.2
  214.9 0.0 copy-start.1
  214.9 1.5 copy.16
  216.4 1.2 copy-done.1
  217.6 0.0 copy-start
  217.6 1.5 copy.17
  219.1 1.2 copy-done
  220.3 1.5 copy.18
Async XLA Ops:
  211.6 3.3 %copy-start.2 = (bf16[2048,640]{1,0:T(8,128)(2,1)S(1)}, bf16[2048,640]{1,0:T(8,128)(2,1)}, u32[]{:S(2)}) copy-start(bf16[2048,640]{1,0:T(8,128)(2,1)} %get-tuple-element.17) | copy-start | bytes 7864324
  214.9 2.7 %copy-start.1 = (bf16[2048,640]{1,0:T(8,128)(2,1)S(1)}, bf16[2048,640]{1,0:T(8,128)(2,1)}, u32[]{:S(2)}) copy-start(bf16[2048,640]{1,0:T(8,128)(2,1)} %get-tuple-element.18) | copy-start | bytes 7864324
  217.6 2.7 %copy-start = (bf16[640,2048]{1,0:T(8,128)(2,1)S(1)}, bf16[640,2048]{1,0:T(8,128)(2,1)}, u32[]{:S(2)}) copy-start(bf16[640,2048]{1,0:T(8,128)(2,1)} %get-tuple-element.19) | copy-start | bytes 7864324

commit v2 on v1

--- a/solution.py
+++ b/solution.py
@@ -11,6 +11,7 @@
 F = 640
 B = 512
 H = 256
+LAST = 128
 F32 = jnp.float32
 BF16 = jnp.bfloat16
 NT = (((1,), (1,)), ((), ()))
@@ -22,8 +23,8 @@
 def kernel(
     x_ref, dy_ref, gate_ref, up_ref, wg_ref, wu_ref, wd_ref,
     dx_ref, dwg_ref, dwu_ref, dwd_ref, dy_all, x_all, rs_in,
-    wd, wgu, dgu, dwd_acc, dwgu_acc, own, tok, gv, uv, dh, hid, p_in, p_out, rs_out,
-    dy_ss, dy_rs, dyp_ss, dyp_rs, x_ss, x_rs, xp_ss, xp_rs, p_ss, p_rs, r_ss, r_rs, w_sem, t_sem, g_sem, o_sem,
+    wd, wgu, dgu, acc, own, tok, gv, uv, dh, hid, p_in, p_out, rs_out, last,
+    dy_ss, dy_rs, dyp_ss, dyp_rs, x_ss, x_rs, xp_ss, xp_rs, p_ss, p_rs, r_ss, r_rs, l_ss, l_rs, w_sem, t_sem, g_sem,
 ):
     me = lax.axis_index("tp")
     core, iy, ix = me % 2, (me // 2) % 2, me // 4
@@ -110,16 +111,19 @@
         w.start()
     for c in gate_copies(0):
         c.start()
-    dwd_acc[...] = jnp.zeros_like(dwd_acc)
-    dwgu_acc[...] = jnp.zeros_like(dwgu_acc)
+    acc[...] = jnp.zeros_like(acc)
     for w in weights:
         w.wait()
 
     def send_p(g):
         return remote(p_out.at[g % 2], p_in.at[g], p_ss.at[g], p_rs.at[g], partner)
 
-    def send_r(stage, slot, dev):
-        return remote(rs_out.at[stage], rs_in.at[slot], r_ss.at[slot], r_rs.at[slot], dev)
+    def send_r(src, slot, dev):
+        return remote(src, rs_in.at[slot], r_ss.at[slot], r_rs.at[slot], dev)
+
+    def send_last(k, i, dev):
+        r = pl.ds(i * LAST, LAST)
+        return remote(rs_out.at[k, r], last.at[k, r], l_ss.at[2 * k + i], l_rs.at[2 * k + i], dev)
 
     def dx_tile(g, r0, j):
         a = dgu[pl.ds(pl.multiple_of(g * B + r0, H), H), :]
@@ -181,7 +185,8 @@
 
         def down(j, carry):
             s = pl.ds(pl.multiple_of(j * 512, 512), 512)
-            dwd_acc[:, s] += lax.dot_general(hid[...], tok[:, s], TN, preferred_element_type=F32)
+            r, c = pl.ds(pl.multiple_of((j // 2) * F, F), F), pl.ds(pl.multiple_of((j % 2) * 512, 512), 512)
+            acc[r, c] += lax.dot_general(hid[...], tok[:, s], TN, preferred_element_type=F32)
             return carry
 
         lax.fori_loop(0, 4, down, 0)
@@ -190,8 +195,6 @@
 
         @pl.when(jnp.logical_or(g < 4, g >= 6))
         def _():
-            stage = jnp.where(g >= 6, g - 4, g % 2)
-
             def m_rows(j, carry):
                 s = pl.ds(pl.multiple_of(j * 512, 512), 512)
                 total = dx_tile(g, H, j) + p_in[g, :, s].astype(F32)
@@ -200,9 +203,13 @@
                 def _():
                     own[pl.ds(pl.multiple_of((g % 2) * H, H), H), s] = total
 
-                @pl.when(g >= 2)
+                @pl.when(jnp.logical_and(g >= 2, g < 4))
                 def _():
-                    rs_out[stage, :, s] = total.astype(BF16)
+                    rs_out[g % 2, :, s] = total.astype(BF16)
+
+                @pl.when(g >= 6)
+                def _():
+                    dx_ref[pl.ds(pl.multiple_of((g % 2) * H, H), H), s] = total.astype(BF16)
 
                 return carry
 
@@ -210,38 +217,27 @@
 
         @pl.when(g == 2)
         def _():
-            send_r(0, 2, nx).start()
+            send_r(rs_out.at[0], 2, nx).start()
 
         @pl.when(g == 3)
         def _():
-            send_r(1, 3, ny).start()
+            send_r(rs_out.at[1], 3, ny).start()
 
         @pl.when(g == 6)
         def _():
-            send_r(2, 0, nx).start()
+            send_r(dx_ref.at[pl.ds(0, H)], 0, nx).start()
 
         @pl.when(g == 7)
         def _():
-            send_r(3, 1, ny).start()
+            send_r(dx_ref.at[pl.ds(H, H)], 1, ny).start()
 
         return carry
 
     lax.fori_loop(0, 8, first_pass, 0)
 
-    def down_out(k, carry):
-        for i in range(5):
-            p_in[i // 2, (i % 2) * 128:(i % 2) * 128 + 128, pl.ds(pl.multiple_of(k * 256, 256), 256)] = dwd_acc[
-                i * 128:i * 128 + 128, pl.ds(pl.multiple_of(k * 256, 256), 256)
-            ].astype(BF16)
-        return carry
-
-    lax.fori_loop(0, 8, down_out, 0)
-    down_copies = [
-        pltpu.make_async_copy(p_in.at[i, pl.ds(0, n)], dwd_ref.at[pl.ds(i * H, n)], o_sem.at[i])
-        for i, n in enumerate((H, H, 128))
-    ]
-    for c in down_copies:
-        c.start()
+    for j in range(4):
+        dwd_ref[:, j * 512:j * 512 + 512] = acc[j // 2 * F:j // 2 * F + F, j % 2 * 512:j % 2 * 512 + 512].astype(BF16)
+    acc[...] = jnp.zeros_like(acc)
 
     relay(x_all, x_ss, x_rs, xp_ss, xp_rs, 2, "y")
     relay(x_all, x_ss, x_rs, xp_ss, xp_rs, 3, "x")
@@ -251,11 +247,6 @@
         c.start()
         return c
 
-    def add_own(pairs):
-        for slot, h in pairs:
-            send_r(0, slot, nx).wait_recv()
-            fetch(slot, h).wait()
-
     def second_pass(g, carry):
         @pl.when(g == 4)
         def _():
@@ -264,7 +255,9 @@
 
         @pl.when(g == 6)
         def _():
-            add_own(((2, 0), (3, 1)))
+            for slot, h in ((2, 0), (3, 1)):
+                send_r(rs_out.at[0], slot, nx).wait_recv()
+                fetch(slot, h).wait()
 
             def add(i, carry):
                 r = pl.ds(pl.multiple_of(i * 32, 32), 32)
@@ -273,10 +266,10 @@
 
             lax.fori_loop(0, B // 32, add, 0)
 
-            send_r(0, 2, nx).wait_send()
-            send_r(1, 3, ny).wait_send()
+            send_r(rs_out.at[0], 2, nx).wait_send()
+            send_r(rs_out.at[1], 3, ny).wait_send()
             for group, slot, k in ((4, 1, 0), (5, 0, 1)):
-                send_r(0, slot, nx).wait_recv()
+                send_r(rs_out.at[0], slot, nx).wait_recv()
                 fetch(slot, k).wait()
 
                 def late(j, carry):
@@ -286,7 +279,10 @@
                     return carry
 
                 lax.fori_loop(0, 4, late, 0)
-                send_r(k, 4 + k, (nx, ny)[k]).start()
+
+            for i in range(H // LAST):
+                send_last(0, i, nx).start()
+                send_last(1, i, ny).start()
 
             relay(x_all, x_ss, x_rs, xp_ss, xp_rs, 6, None)
             relay(x_all, x_ss, x_rs, xp_ss, xp_rs, 7, None)
@@ -297,7 +293,7 @@
         def weight(j, carry):
             s = pl.ds(pl.multiple_of(j * 512, 512), 512)
             d = dgu[pl.ds(pl.multiple_of(g * B, B), B), :]
-            dwgu_acc[s, :] += lax.dot_general(tok[:, s], d, TN, preferred_element_type=F32)
+            acc[s, :] += lax.dot_general(tok[:, s], d, TN, preferred_element_type=F32)
             return carry
 
         lax.fori_loop(0, 4, weight, 0)
@@ -307,30 +303,26 @@
 
     def weight_out(i, carry):
         r = pl.ds(pl.multiple_of(i * 32, 32), 32)
-        dgu[r, :] = dwgu_acc[r, :].astype(BF16)
+        dwg_ref[r, :] = acc[r, 0:F].astype(BF16)
+        dwu_ref[r, :] = acc[r, F:2 * F].astype(BF16)
         return carry
 
     lax.fori_loop(0, D // 32, weight_out, 0)
-    weight_copies = (
-        pltpu.make_async_copy(dgu.at[pl.ds(0, D), pl.ds(0, F)], dwg_ref, o_sem.at[3]),
-        pltpu.make_async_copy(dgu.at[pl.ds(0, D), pl.ds(F, F)], dwu_ref, o_sem.at[4]),
-    )
-    for c in weight_copies:
-        c.start()
-
-    add_own(((5, 0), (4, 1)))
-
-    def finish(i, carry):
-        r = pl.ds(pl.multiple_of(i * 32, 32), 32)
-        tok[r, :] = (own[r, :] + tok[r, :].astype(F32)).astype(BF16)
-        return carry
-
-    lax.fori_loop(0, B // 32, finish, 0)
-    out = pltpu.make_async_copy(tok, dx_ref, o_sem.at[5])
-    out.start()
-
-    for c in down_copies + list(weight_copies) + [out]:
-        c.wait()
+
+    send_r(dx_ref.at[pl.ds(0, H)], 0, nx).wait_send()
+    send_r(dx_ref.at[pl.ds(H, H)], 1, ny).wait_send()
+    for i in range(H // LAST):
+        for k in range(2):
+            send_last(k, i, nx).wait_recv()
+
+            def finish(n, carry):
+                q = pl.ds(pl.multiple_of(i * LAST + n * 32, 32), 32)
+                r = pl.ds(pl.multiple_of((1 - k) * H + i * LAST + n * 32, 32), 32)
+                dx_ref[r, :] = (own[r, :] + last[k, q, :].astype(F32)).astype(BF16)
+                return carry
+
+            lax.fori_loop(0, LAST // 32, finish, 0)
+
     for full, ss, rs, pss, prs in ((dy_all, dy_ss, dy_rs, dyp_ss, dyp_rs), (x_all, x_ss, x_rs, xp_ss, xp_rs)):
         for g in range(8):
             send_on(full, pss, prs, g, g, partner).wait_send()
@@ -338,25 +330,25 @@
                 send_on(full, ss, rs, g, g, partner).wait_send()
     for g in (6, 7):
         send_p(g).wait_send()
-    for stage, slot in ((2, 0), (3, 1), (0, 4), (1, 5)):
-        send_r(stage, slot, nx).wait_send()
+    for i in range(H // LAST):
+        send_last(0, i, nx).wait_send()
+        send_last(1, i, ny).wait_send()
 
 
 def solution(mesh):
     def local(*args):
         any_ = pl.BlockSpec(memory_space=pl.ANY)
         dma = pltpu.SemaphoreType.DMA
-        shapes = [(B, D), (D, F), (D, F), (F, D), (8 * B, D), (8 * B, D), (6, H, D)]
+        shapes = [(B, D), (D, F), (D, F), (F, D), (8 * B, D), (8 * B, D), (4, H, D)]
         outs = pl.pallas_call(
             kernel,
-            out_shape=[jax.ShapeDtypeStruct(s, BF16) for s in shapes],
+            out_shape=[pltpu.VMEM(s, BF16) for s in shapes[:4]] + [jax.ShapeDtypeStruct(s, BF16) for s in shapes[4:]],
             in_specs=[any_] * 7,
-            out_specs=[any_] * 7,
+            out_specs=[pl.BlockSpec(memory_space=pltpu.VMEM)] * 4 + [any_] * 3,
             scratch_shapes=[
                 pltpu.VMEM((F, D), BF16),
                 pltpu.VMEM((D, 2 * F), BF16),
                 pltpu.VMEM((8 * B, 2 * F), BF16),
-                pltpu.VMEM((F, D), F32),
                 pltpu.VMEM((D, 2 * F), F32),
                 pltpu.VMEM((B, D), F32),
                 pltpu.VMEM((B, D), BF16),
@@ -366,11 +358,12 @@
                 pltpu.VMEM((B, F), BF16),
                 pltpu.VMEM((8, H, D), BF16),
                 pltpu.VMEM((2, H, D), BF16),
-                pltpu.VMEM((4, H, D), BF16),
+                pltpu.VMEM((2, H, D), BF16),
+                pltpu.VMEM((2, H, D), BF16),
             ]
             + [dma((8,))] * 12
-            + [dma((3,)), dma((2,)), dma((4,)), dma((6,))],
-            compiler_params=pltpu.CompilerParams(collective_id=0, has_side_effects=True, vmem_limit_bytes=67043328),
+            + [dma((4,)), dma((4,)), dma((3,)), dma((2,)), dma((4,))],
+            compiler_params=pltpu.CompilerParams(collective_id=0, has_side_effects=True, vmem_limit_bytes=53*1048576),
             name="backward",
         )(*args)
         return tuple(outs[:4])

time: 224 us -> 216 us (0.964)
  local copies, waits for them, and re-layouts: 10.2 us -> 5.79 us
  Pallas kernels: 211 us -> 207 us
    unnamed x10 -> x4, local copies, waits for them, and re-layouts: 10.2 us -> 5.79 us
    pallas_call x1, Pallas kernels: 211 us -> 207 us  [local(): pl.pallas_call(kernel, out_shape=[pltpu.VMEM(s, BF16) for s in shapes[:4]...]
where the time goes in v2:
time: 216 us; the launch traced here: 213 us
  Pallas kernels  207 us (96%)
  local copies, waits for them, and re-layouts  5.79 us (3%)
    pallas_call x1, Pallas kernels, local(): pl.pallas_call(kernel, out_shape=[pltpu.VMEM(s, BF16) for s in shapes[:4]...  207 us
    unnamed x4, local copies, waits for them, and re-layouts  5.79 us

profile of v2, /device:TPU:1, one launch (start us, length us, event | category | flops | bytes accessed | tf_op | source)
XLA Modules:
  0.0 213.4 jit_solution(4489968308473031972)
XLA Ops:
  0.6 206.9 %backward.1 = (bf16[512,2048]{1,0:T(8,128)(2,1)S(1)}, bf16[2048,640]{1,0:T(8,128)(2,1)S(1)}, bf16[2048,640]{1,0:T(8,128)(2,1)S(1)}, bf16[640,2048]{1,0:T(8,128)(...) custom-call(bf16[512,2048]{1,0:T(8,128)(2,1)} %x_ref.1, ...), custom_call_target="tpu_custom_call" | custom-call | tf_op jit(solution)/shard_map/backward/pallas_call | solution.py:343
  207.6 1.3 copy.15
  208.9 1.5 copy.16
  210.4 1.5 copy.17
  211.9 1.5 copy.18

commit v3 on v2

--- a/solution.py
+++ b/solution.py
@@ -22,8 +22,8 @@
 
 def kernel(
     x_ref, dy_ref, gate_ref, up_ref, wg_ref, wu_ref, wd_ref,
-    dx_ref, dwg_ref, dwu_ref, dwd_ref, dy_all, x_all, rs_in,
-    wd, wgu, dgu, acc, own, tok, gv, uv, dh, hid, p_in, p_out, rs_out, last,
+    own, last, dwg_ref, dwu_ref, dwd_ref, dy_all, x_all, rs_in,
+    wd, wgu, dgu, acc, tok, gv, uv, dh, hid, p_in, p_out, rs_out,
     dy_ss, dy_rs, dyp_ss, dyp_rs, x_ss, x_rs, xp_ss, xp_rs, p_ss, p_rs, r_ss, r_rs, l_ss, l_rs, w_sem, t_sem, g_sem,
 ):
     me = lax.axis_index("tp")
@@ -203,13 +203,9 @@
                 def _():
                     own[pl.ds(pl.multiple_of((g % 2) * H, H), H), s] = total
 
-                @pl.when(jnp.logical_and(g >= 2, g < 4))
+                @pl.when(g >= 2)
                 def _():
-                    rs_out[g % 2, :, s] = total.astype(BF16)
-
-                @pl.when(g >= 6)
-                def _():
-                    dx_ref[pl.ds(pl.multiple_of((g % 2) * H, H), H), s] = total.astype(BF16)
+                    rs_out[jnp.where(g >= 6, g - 4, g % 2), :, s] = total.astype(BF16)
 
                 return carry
 
@@ -225,11 +221,11 @@
 
         @pl.when(g == 6)
         def _():
-            send_r(dx_ref.at[pl.ds(0, H)], 0, nx).start()
+            send_r(rs_out.at[2], 0, nx).start()
 
         @pl.when(g == 7)
         def _():
-            send_r(dx_ref.at[pl.ds(H, H)], 1, ny).start()
+            send_r(rs_out.at[3], 1, ny).start()
 
         return carry
 
@@ -309,20 +305,11 @@
 
     lax.fori_loop(0, D // 32, weight_out, 0)
 
-    send_r(dx_ref.at[pl.ds(0, H)], 0, nx).wait_send()
-    send_r(dx_ref.at[pl.ds(H, H)], 1, ny).wait_send()
+    send_r(rs_out.at[2], 0, nx).wait_send()
+    send_r(rs_out.at[3], 1, ny).wait_send()
     for i in range(H // LAST):
         for k in range(2):
             send_last(k, i, nx).wait_recv()
-
-            def finish(n, carry):
-                q = pl.ds(pl.multiple_of(i * LAST + n * 32, 32), 32)
-                r = pl.ds(pl.multiple_of((1 - k) * H + i * LAST + n * 32, 32), 32)
-                dx_ref[r, :] = (own[r, :] + last[k, q, :].astype(F32)).astype(BF16)
-                return carry
-
-            lax.fori_loop(0, LAST // 32, finish, 0)
-
     for full, ss, rs, pss, prs in ((dy_all, dy_ss, dy_rs, dyp_ss, dyp_rs), (x_all, x_ss, x_rs, xp_ss, xp_rs)):
         for g in range(8):
             send_on(full, pss, prs, g, g, partner).wait_send()
@@ -335,22 +322,47 @@
         send_last(1, i, ny).wait_send()
 
 
+def finish(own, last, dwg, dwu, dwd, dx_ref, dwg_ref, dwu_ref, dwd_ref, dx, sem, dx_sem):
+    copies = [
+        pltpu.make_async_copy(src, dst, sem.at[i])
+        for i, (src, dst) in enumerate(((dwd, dwd_ref), (dwg, dwg_ref), (dwu, dwu_ref)))
+    ]
+    for c in copies:
+        c.start()
+    for q in range(B // LAST):
+        k, i = 1 - q * LAST // H, q * LAST % H
+
+        def add(n, carry):
+            r = pl.ds(pl.multiple_of(q * LAST + n * 32, 32), 32)
+            dx[r, :] = (own[r, :] + last[k, pl.ds(pl.multiple_of(i + n * 32, 32), 32), :].astype(F32)).astype(BF16)
+            return carry
+
+        lax.fori_loop(0, LAST // 32, add, 0)
+        r = pl.ds(q * LAST, LAST)
+        copies.append(pltpu.make_async_copy(dx.at[r], dx_ref.at[r], dx_sem.at[q]))
+        copies[-1].start()
+    for c in copies:
+        c.wait()
+
+
 def solution(mesh):
     def local(*args):
         any_ = pl.BlockSpec(memory_space=pl.ANY)
         dma = pltpu.SemaphoreType.DMA
-        shapes = [(B, D), (D, F), (D, F), (F, D), (8 * B, D), (8 * B, D), (4, H, D)]
-        outs = pl.pallas_call(
+        vmem = pl.BlockSpec(memory_space=pltpu.VMEM)
+        grads = [(D, F), (D, F), (F, D)]
+        kept = pl.pallas_call(
             kernel,
-            out_shape=[pltpu.VMEM(s, BF16) for s in shapes[:4]] + [jax.ShapeDtypeStruct(s, BF16) for s in shapes[4:]],
+            out_shape=[pltpu.VMEM((B, D), F32), pltpu.VMEM((2, H, D), BF16)]
+            + [pltpu.VMEM(s, BF16) for s in grads]
+            + [jax.ShapeDtypeStruct(s, BF16) for s in ((8 * B, D), (8 * B, D), (4, H, D))],
             in_specs=[any_] * 7,
-            out_specs=[pl.BlockSpec(memory_space=pltpu.VMEM)] * 4 + [any_] * 3,
+            out_specs=[vmem] * 5 + [any_] * 3,
             scratch_shapes=[
                 pltpu.VMEM((F, D), BF16),
                 pltpu.VMEM((D, 2 * F), BF16),
                 pltpu.VMEM((8 * B, 2 * F), BF16),
                 pltpu.VMEM((D, 2 * F), F32),
-                pltpu.VMEM((B, D), F32),
                 pltpu.VMEM((B, D), BF16),
                 pltpu.VMEM((B, F), BF16),
                 pltpu.VMEM((B, F), BF16),
@@ -358,15 +370,24 @@
                 pltpu.VMEM((B, F), BF16),
                 pltpu.VMEM((8, H, D), BF16),
                 pltpu.VMEM((2, H, D), BF16),
-                pltpu.VMEM((2, H, D), BF16),
-                pltpu.VMEM((2, H, D), BF16),
+                pltpu.VMEM((4, H, D), BF16),
             ]
             + [dma((8,))] * 12
             + [dma((4,)), dma((4,)), dma((3,)), dma((2,)), dma((4,))],
-            compiler_params=pltpu.CompilerParams(collective_id=0, has_side_effects=True, vmem_limit_bytes=53*1048576),
+            compiler_params=pltpu.CompilerParams(collective_id=0, has_side_effects=True, vmem_limit_bytes=49 * 2**20),
             name="backward",
         )(*args)
-        return tuple(outs[:4])
+        return tuple(
+            pl.pallas_call(
+                finish,
+                out_shape=[jax.ShapeDtypeStruct(s, BF16) for s in [(B, D), *grads]],
+                in_specs=[vmem] * 5,
+                out_specs=[any_] * 4,
+                scratch_shapes=[pltpu.VMEM((B, D), BF16), dma((3,)), dma((B // LAST,))],
+                compiler_params=pltpu.CompilerParams(vmem_limit_bytes=24 * 2**20),
+                name="finish",
+            )(*kept[:5])
+        )
 
     rows, cols = P(("dp", "tp"), None), P("dp", "tp")
     return jax.shard_map(

time: 216 us -> 214 us (level)
  local copies, waits for them, and re-layouts: 5.79 us -> 0 us
  Pallas kernels: 207 us -> 211 us
    unnamed x4 -> x0, local copies, waits for them, and re-layouts: 5.79 us -> none
    pallas_call x1 -> x2, Pallas kernels: 207 us -> 211 us  [the longest x1 207 us: local(): pl.pallas_call(kernel, out_shape=[pltpu.VMEM((B, D), F32), pltpu.VMEM((2,...]
where the time goes in v3:
time: 214 us; the launch traced here: 211 us
  Pallas kernels  211 us (99%)
    pallas_call x1, Pallas kernels, local(): pl.pallas_call(kernel, out_shape=[pltpu.VMEM((B, D), F32), pltpu.VMEM((2,...  207 us

profile of v3, /device:TPU:1, one launch (start us, length us, event | category | flops | bytes accessed | tf_op | source)
XLA Modules:
  0.0 211.2 jit_solution(8581918176716118696)
XLA Ops:
  0.6 206.7 %backward.1 = (f32[512,2048]{1,0:T(8,128)S(1)}, bf16[2,256,2048]{2,1,0:T(8,128)(2,1)S(1)}, bf16[2048,640]{1,0:T(8,128)(2,1)S(1)}, bf16[2048,640]{1,0:T(8,128)(2,...) custom-call(bf16[512,2048]{1,0:T(8,128)(2,1)} %x_ref.1, ...), custom_call_target="tpu_custom_call" | custom-call | tf_op jit(solution)/shard_map/backward/pallas_call | solution.py:354
  207.4 3.8 %finish.1 = (bf16[512,2048]{1,0:T(8,128)(2,1)}, bf16[2048,640]{1,0:T(8,128)(2,1)}, bf16[2048,640]{1,0:T(8,128)(2,1)}, bf16[640,2048]{1,0:T(8,128)(2,1)}) custom-call(f32[512,2048]{1,0:T(8,128)S(1)} %get-tuple-element.9.own, bf16[2,256,2048]{2,1,0:T(8,128)(2,1)S(1)} %get-tuple-element.10.last, bf16[2048,640]{1,0:T(8,128)(2,1)S(1)} %get-tuple-element.11.dwg, ...), custom_call_target="tpu_custom_call" | custom-call | tf_op jit(solution)/shard_map/finish/pallas_call | solution.py:381

commit v4 on v3

--- a/solution.py
+++ b/solution.py
@@ -11,7 +11,8 @@
 F = 640
 B = 512
 H = 256
-LAST = 128
+LAST = 256
+SHIFT = 32
 F32 = jnp.float32
 BF16 = jnp.bfloat16
 NT = (((1,), (1,)), ((), ()))
@@ -24,7 +25,7 @@
     x_ref, dy_ref, gate_ref, up_ref, wg_ref, wu_ref, wd_ref,
     own, last, dwg_ref, dwu_ref, dwd_ref, dy_all, x_all, rs_in,
     wd, wgu, dgu, acc, tok, gv, uv, dh, hid, p_in, p_out, rs_out,
-    dy_ss, dy_rs, dyp_ss, dyp_rs, x_ss, x_rs, xp_ss, xp_rs, p_ss, p_rs, r_ss, r_rs, l_ss, l_rs, w_sem, t_sem, g_sem,
+    dy_ss, dy_rs, dyp_ss, dyp_rs, x_ss, x_rs, xp_ss, xp_rs, p_ss, p_rs, r_ss, r_rs, l_ss, l_rs, e_ss, e_rs, ep_ss, ep_rs, w_sem, t_sem, g_sem,
 ):
     me = lax.axis_index("tp")
     core, iy, ix = me % 2, (me // 2) % 2, me // 4
@@ -123,7 +124,7 @@
 
     def send_last(k, i, dev):
         r = pl.ds(i * LAST, LAST)
-        return remote(rs_out.at[k, r], last.at[k, r], l_ss.at[2 * k + i], l_rs.at[2 * k + i], dev)
+        return remote(rs_out.at[k, r], last.at[k, r], l_ss.at[k * (H // LAST) + i], l_rs.at[k * (H // LAST) + i], dev)
 
     def dx_tile(g, r0, j):
         a = dgu[pl.ds(pl.multiple_of(g * B + r0, H), H), :]
@@ -235,8 +236,45 @@
         dwd_ref[:, j * 512:j * 512 + 512] = acc[j // 2 * F:j // 2 * F + F, j % 2 * 512:j % 2 * 512 + 512].astype(BF16)
     acc[...] = jnp.zeros_like(acc)
 
-    relay(x_all, x_ss, x_rs, xp_ss, xp_rs, 2, "y")
-    relay(x_all, x_ss, x_rs, xp_ss, xp_rs, 3, "x")
+    def onward(k, n):
+        g = 2 + k
+        r = pl.ds(pl.multiple_of(owner(g) * B + half(g) * H, H), n)
+        return remote(x_all.at[r], x_all.at[r], x_ss.at[6 + k], x_rs.at[6 + k], (ny, nx)[k])
+
+    def tail(g):
+        return pl.ds(pl.multiple_of((owner(g) - core) * B + half(g) * H + H - SHIFT, 8), SHIFT)
+
+    def onward_tail(k):
+        r = tail(2 + k)
+        return remote(x_all.at[r], x_all.at[r], e_ss.at[k], e_rs.at[k], (ny, nx)[k])
+
+    def to_partner(k, n):
+        g = 6 + k
+        r = pl.ds(pl.multiple_of(owner(g) * B + half(g) * H, H), n)
+        return remote(x_all.at[r], x_all.at[r], xp_ss.at[g], xp_rs.at[g], partner)
+
+    def to_partner_tail(k):
+        r = tail(6 + k)
+        return remote(x_all.at[r], x_all.at[r], ep_ss.at[k], ep_rs.at[k], partner)
+
+    for k in range(2):
+        arrived(x_all, x_ss, x_rs, 2 + k)
+
+        @pl.when(core == 0)
+        def _():
+            onward(k, H - SHIFT).start()
+
+        @pl.when(core == 1)
+        def _():
+            onward(k, H).start()
+
+        send_on(x_all, xp_ss, xp_rs, 2 + k, 2 + k, partner).start()
+    for k in range(2):
+        arrived(x_all, xp_ss, xp_rs, 2 + k)
+
+        @pl.when(core == 1)
+        def _():
+            onward_tail(k).start()
 
     def fetch(slot, k):
         c = pltpu.make_async_copy(rs_in.at[slot], tok.at[pl.ds(k * H, H)], t_sem.at[k])
@@ -280,10 +318,30 @@
                 send_last(0, i, nx).start()
                 send_last(1, i, ny).start()
 
-            relay(x_all, x_ss, x_rs, xp_ss, xp_rs, 6, None)
-            relay(x_all, x_ss, x_rs, xp_ss, xp_rs, 7, None)
-
-        arrived(x_all, xp_ss, xp_rs, g)
+            @pl.when(core == 0)
+            def _():
+                for k in range(2):
+                    onward(k, H - SHIFT).wait_recv()
+                    to_partner(k, H - SHIFT).start()
+                for k in range(2):
+                    to_partner(k, H).wait_recv()
+                    to_partner_tail(k).wait_recv()
+
+            @pl.when(core == 1)
+            def _():
+                for k in range(2):
+                    onward(k, H).wait_recv()
+                    to_partner(k, H).start()
+                for k in range(2):
+                    onward_tail(k).wait_recv()
+                    to_partner_tail(k).start()
+                for k in range(2):
+                    to_partner(k, H - SHIFT).wait_recv()
+
+        @pl.when(jnp.logical_or(g < 2, jnp.logical_or(g == 4, g == 5)))
+        def _():
+            arrived(x_all, xp_ss, xp_rs, g)
+
         load_tokens(x_ref, x_all, g)
 
         def weight(j, carry):
@@ -307,19 +365,37 @@
 
     send_r(rs_out.at[2], 0, nx).wait_send()
     send_r(rs_out.at[3], 1, ny).wait_send()
-    for i in range(H // LAST):
-        for k in range(2):
-            send_last(k, i, nx).wait_recv()
-    for full, ss, rs, pss, prs in ((dy_all, dy_ss, dy_rs, dyp_ss, dyp_rs), (x_all, x_ss, x_rs, xp_ss, xp_rs)):
-        for g in range(8):
+    for full, ss, rs, pss, prs, n in (
+        (dy_all, dy_ss, dy_rs, dyp_ss, dyp_rs, 8),
+        (x_all, x_ss, x_rs, xp_ss, xp_rs, 6),
+    ):
+        for g in range(n):
             send_on(full, pss, prs, g, g, partner).wait_send()
             if g >= 2:
                 send_on(full, ss, rs, g, g, partner).wait_send()
     for g in (6, 7):
         send_p(g).wait_send()
+
+    @pl.when(core == 0)
+    def _():
+        for k in range(2):
+            onward(k, H - SHIFT).wait_send()
+            to_partner(k, H - SHIFT).wait_send()
+
+    @pl.when(core == 1)
+    def _():
+        for k in range(2):
+            onward(k, H).wait_send()
+            to_partner(k, H).wait_send()
+            onward_tail(k).wait_send()
+            to_partner_tail(k).wait_send()
+
     for i in range(H // LAST):
-        send_last(0, i, nx).wait_send()
-        send_last(1, i, ny).wait_send()
+        for k in range(2):
+            send_last(k, i, nx).wait_send()
+    for i in range(H // LAST):
+        for k in range(2):
+            send_last(k, i, nx).wait_recv()
 
 
 def finish(own, last, dwg, dwu, dwd, dx_ref, dwg_ref, dwu_ref, dwd_ref, dx, sem, dx_sem):
@@ -373,7 +449,9 @@
                 pltpu.VMEM((4, H, D), BF16),
             ]
             + [dma((8,))] * 12
-            + [dma((4,)), dma((4,)), dma((3,)), dma((2,)), dma((4,))],
+            + [dma((2 * H // LAST,))] * 2
+            + [dma((2,))] * 4
+            + [dma((3,)), dma((2,)), dma((4,))],
             compiler_params=pltpu.CompilerParams(collective_id=0, has_side_effects=True, vmem_limit_bytes=49 * 2**20),
             name="backward",
         )(*args)

time: 214 us -> 213 us (level)
  no operation moved by 1% of the time
where the time goes in v4:
time: 213 us; the launch traced here: 212 us
  Pallas kernels  211 us (99%)
    pallas_call x1, Pallas kernels, local(): pl.pallas_call(kernel, out_shape=[pltpu.VMEM((B, D), F32), pltpu.VMEM((2,...  208 us

profile of v4, /device:TPU:1, one launch (start us, length us, event | category | flops | bytes accessed | tf_op | source)
XLA Modules:
  0.0 212.0 jit_solution(1827205360931067784)
XLA Ops:
  0.6 207.6 %backward.1 = (f32[512,2048]{1,0:T(8,128)S(1)}, bf16[2,256,2048]{2,1,0:T(8,128)(2,1)S(1)}, bf16[2048,640]{1,0:T(8,128)(2,1)S(1)}, bf16[2048,640]{1,0:T(8,128)(2,...) custom-call(bf16[512,2048]{1,0:T(8,128)(2,1)} %x_ref.1, ...), custom_call_target="tpu_custom_call" | custom-call | tf_op jit(solution)/shard_map/backward/pallas_call | solution.py:430
  208.2 3.8 %finish.1 = (bf16[512,2048]{1,0:T(8,128)(2,1)}, bf16[2048,640]{1,0:T(8,128)(2,1)}, bf16[2048,640]{1,0:T(8,128)(2,1)}, bf16[640,2048]{1,0:T(8,128)(2,1)}) custom-call(f32[512,2048]{1,0:T(8,128)S(1)} %get-tuple-element.9.own, bf16[2,256,2048]{2,1,0:T(8,128)(2,1)S(1)} %get-tuple-element.10.last, bf16[2048,640]{1,0:T(8,128)(2,1)S(1)} %get-tuple-element.11.dwg, ...), custom_call_target="tpu_custom_call" | custom-call | tf_op jit(solution)/shard_map/finish/pallas_call | solution.py:459

commit v5 on v3

v5 whole, which is shorter than its diff:
```python
import functools

import jax
import jax.numpy as jnp
from jax import lax
from jax.experimental import pallas as pl
from jax.experimental.pallas import tpu as pltpu
from jax.sharding import PartitionSpec as P

D = 2048
F = 640
B = 512
H = 256
LAST = 128
SHIFT = 32
F32 = jnp.float32
BF16 = jnp.bfloat16
NT = (((1,), (1,)), ((), ()))
TN = (((0,), (0,)), ((), ()))
C0 = 0.7978845608028654
C1 = 0.7978845608028654 * 0.044715


def kernel(
    x_ref, dy_ref, gate_ref, up_ref, wg_ref, wu_ref, wd_ref,
    own, last, dwg_ref, dwu_ref, dwd_ref, dy_all, x_all, rs_in,
    wd, wgu, dgu, acc, tok, guv, dh, hid, p_in, p_out, rs_out,
    dy_s, dy_r, dyp_r, x_s, x_r, xp_r, p_s, p_r, r_s, r_r, l_s, l_r, w_sem, t_sem, g_sem,
):
    me = lax.axis_index("tp")
    core, iy, ix = me % 2, (me // 2) % 2, me // 4
    other = 1 - 2 * core
    partner = me + other
    ny = me + 2 - 4 * iy
    nx = me + 4 - 8 * ix
    nd = ny + 4 - 8 * ix

    barrier = pltpu.get_barrier_semaphore()
    for d in (partner, nx, ny):
        pl.semaphore_signal(barrier, inc=1, device_id={"tp": d}, device_id_type=pl.DeviceIdType.MESH)
    pl.semaphore_wait(barrier, 3)

    def owner(g):
        return jnp.where(g < 2, me, jnp.where(g >= 6, nd, jnp.where(g % 2 == 0, nx, ny)))

    def half(g):
        return jnp.where(g == 4, 1, jnp.where(g == 5, 0, g % 2))

    def rows(dev, h, n=H):
        return pl.ds(pl.multiple_of(dev * B + h * H, H), n)

    def remote(src, dst, ss, rs, dev):
        return pltpu.make_async_remote_copy(
            src_ref=src, dst_ref=dst, send_sem=ss, recv_sem=rs, device_id={"tp": dev}, device_id_type=pl.DeviceIdType.MESH
        )

    def of_rows(full, n, ss, rs):
        return remote(full.at[pl.ds(0, n)], full.at[pl.ds(0, n)], ss, rs, partner)

    def start_own(ref, full, s, r, pr):
        for h, p, dev in ((0, 0, nx), (1, 0, ny), (0, None, partner), (1, 1, nx), (0, 1, ny), (1, None, partner)):
            remote(ref.at[pl.ds(h * H, H)], full.at[rows(me, h)], s.at[0], pr.at[0] if p is None else r.at[p], dev).start()

    def send_on(full, s, r, g, n, dev):
        q = rows(owner(g), half(g), n)
        remote(full.at[q], full.at[q], s.at[0], r, dev).start()

    def relay(full, s, r, pr, p, onward):
        of_rows(full, 2 * H, s.at[0], r.at[p - 1]).wait_recv()
        if onward:
            send_on(full, s, r.at[2], 2, H, ny)
            send_on(full, s, r.at[2], 3, H, nx)
        for g in (2 * p, 2 * p + 1):
            send_on(full, s, pr.at[p], g, H, partner)

    def from_partner(full, s, pr, p):
        of_rows(full, 2 * H, s.at[0], pr.at[p]).wait_recv()

    def load(ref, full, g):
        o, h, slot = owner(g), half(g), g % 2
        pltpu.make_async_copy(full.at[rows(o + other, h)], tok.at[slot, pl.ds(0, H)], t_sem.at[slot]).start()

        @pl.when(g < 2)
        def _():
            src = ref.at[pl.ds(pl.multiple_of(h * H, H), H)]
            pltpu.make_async_copy(src, tok.at[slot, pl.ds(H, H)], t_sem.at[slot]).start()

        @pl.when(g >= 2)
        def _():
            pltpu.make_async_copy(full.at[rows(o, h)], tok.at[slot, pl.ds(H, H)], t_sem.at[slot]).start()

    def loaded(slot):
        pltpu.make_async_copy(dy_all.at[pl.ds(0, B)], tok.at[slot], t_sem.at[slot]).wait()

    def load_gates(g):
        o, h = owner(g), half(g)
        for i, src in enumerate((gate_ref, up_ref)):
            pltpu.make_async_copy(src.at[rows(o + other, h)], guv.at[i, pl.ds(0, H)], g_sem.at[0]).start()
            pltpu.make_async_copy(src.at[rows(o, h)], guv.at[i, pl.ds(H, H)], g_sem.at[0]).start()

    start_own(dy_ref, dy_all, dy_s, dy_r, dyp_r)
    pltpu.make_async_copy(wd_ref, wd, w_sem.at[0]).start()
    load_gates(0)
    pltpu.make_async_copy(wg_ref, wgu.at[:, pl.ds(0, F)], w_sem.at[1]).start()
    pltpu.make_async_copy(wu_ref, wgu.at[:, pl.ds(F, F)], w_sem.at[1]).start()
    from_partner(dy_all, dy_s, dyp_r, 0)
    load(dy_ref, dy_all, 0)
    acc[...] = jnp.zeros_like(acc)
    pltpu.make_async_copy(wd_ref, wd, w_sem.at[0]).wait()
    pltpu.make_async_copy(wgu, wgu, w_sem.at[1]).wait()

    def p_slot(g):
        return jnp.where(jnp.logical_or(g == 4, g == 5), g - 2, g % 2)

    def send_p(g):
        return remote(p_out.at[g % 2], p_in.at[p_slot(g)], p_s.at[g % 2], p_r.at[g % 2], partner)

    def send_r(stage, kind, k, dev):
        return remote(rs_out.at[stage], rs_in.at[kind, pl.ds(k * H, H)], r_s.at[kind], r_r.at[kind], dev)

    def both_r(kind):
        return remote(rs_in.at[kind], rs_in.at[kind], r_s.at[kind], r_r.at[kind], nx)

    def send_last(k, dev):
        return remote(rs_out.at[k], last.at[k], l_s.at[0], l_r.at[0], dev)

    def dx_tile(g, r0, j):
        a = dgu[pl.ds(pl.multiple_of(g * B + r0, H), H), :]
        w = wgu[pl.ds(pl.multiple_of(j * 512, 512), 512), :]
        return lax.dot_general(a, w, NT, preferred_element_type=F32)

    def first_pass(g, carry):
        slot = g % 2
        loaded(slot)
        pltpu.make_async_copy(guv, guv, g_sem.at[0]).wait()

        @pl.when(slot == 0)
        def _():
            load(dy_ref, dy_all, g + 1)

        for n0, n in ((0, 256), (256, 256), (512, 128)):
            dh[:, n0:n0 + n] = lax.dot_general(tok[slot], wd[n0:n0 + n, :], NT, preferred_element_type=F32)

        def gates(i, carry):
            r = pl.ds(pl.multiple_of(i * 32, 32), 32)
            a, u, d = guv[0, r, :].astype(F32), guv[1, r, :].astype(F32), dh[r, :]
            a2 = a * a
            t = jnp.tanh(a * (C0 + C1 * a2))
            cdf = 0.5 + 0.5 * t
            gelu = a * cdf
            slope = cdf + (0.5 * a) * ((1.0 - t * t) * (C0 + (3.0 * C1) * a2))
            hid[r, :] = (gelu * u).astype(BF16)
            q = pl.ds(pl.multiple_of(g * B + i * 32, 32), 32)
            dgu[q, 0:F] = (d * u * slope).astype(BF16)
            dgu[q, F:2 * F] = (d * gelu).astype(BF16)
            return carry

        lax.fori_loop(0, B // 32, gates, 0)

        @pl.when(g < 7)
        def _():
            load_gates(g + 1)

        @pl.when(g >= 2)
        def _():
            send_p(g - 2).wait_send()

        def p_rows(j, carry):
            p_out[slot, :, pl.ds(pl.multiple_of(j * 512, 512), 512)] = dx_tile(g, 0, j).astype(BF16)
            return carry

        lax.fori_loop(0, 4, p_rows, 0)
        send_p(g).start()

        def down(j, carry):
            s = pl.ds(pl.multiple_of(j * 512, 512), 512)
            r, c = pl.ds(pl.multiple_of((j // 2) * F, F), F), pl.ds(pl.multiple_of((j % 2) * 512, 512), 512)
            acc[r, c] += lax.dot_general(hid[...], tok[slot, :, s], TN, preferred_element_type=F32)
            return carry

        lax.fori_loop(0, 4, down, 0)

        for p in (1, 2, 3):
            @pl.when(g == 2 * p - 1)
            def _():
                relay(dy_all, dy_s, dy_r, dyp_r, p, p == 1)
                if p == 1:
                    start_own(x_ref, x_all, x_s, x_r, xp_r)
                from_partner(dy_all, dy_s, dyp_r, p)
                load(dy_ref, dy_all, g + 1)

        @pl.when(g == 7)
        def _():
            from_partner(x_all, x_s, xp_r, 0)
            load(x_ref, x_all, 0)

        send_p(g).wait_recv()

        @pl.when(jnp.logical_or(g < 4, g >= 6))
        def _():
            def m_rows(j, carry):
                s = pl.ds(pl.multiple_of(j * 512, 512), 512)
                total = dx_tile(g, H, j) + p_in[p_slot(g), :, s].astype(F32)

                @pl.when(g < 2)
                def _():
                    own[pl.ds(pl.multiple_of(slot * H, H), H), s] = total

                @pl.when(g >= 2)
                def _():
                    rs_out[jnp.where(g >= 6, g - 4, slot), :, s] = total.astype(BF16)

                return carry

            lax.fori_loop(0, 4, m_rows, 0)

        for group, stage, kind, k, dev in ((2, 0, 0, 0, nx), (3, 1, 0, 1, ny), (6, 2, 1, 1, nx), (7, 3, 1, 0, ny)):
            @pl.when(g == group)
            def _():
                send_r(stage, kind, k, dev).start()

        return carry

    lax.fori_loop(0, 8, first_pass, 0)

    for j in range(4):
        dwd_ref[:, j * 512:j * 512 + 512] = acc[j // 2 * F:j // 2 * F + F, j % 2 * 512:j % 2 * 512 + 512].astype(BF16)
    acc[...] = jnp.zeros_like(acc)

    def tail(g):
        return pl.ds(pl.multiple_of((owner(g) - core) * B + half(g) * H + H - SHIFT, 8), SHIFT)

    def send_tail(g, r, dev):
        remote(x_all.at[tail(g)], x_all.at[tail(g)], x_s.at[0], r, dev).start()

    def second_pass(g, carry):
        slot = g % 2
        loaded(slot)

        @pl.when(slot == 0)
        def _():
            load(x_ref, x_all, g + 1)

        @pl.when(g == 1)
        def _():
            relay(x_all, x_s, x_r, xp_r, 1, False)
            for c, n in ((0, H - SHIFT), (1, H)):
                @pl.when(core == c)
                def _():
                    send_on(x_all, x_s, x_r.at[2], 2, n, ny)
                    send_on(x_all, x_s, x_r.at[2], 3, n, nx)

            from_partner(x_all, x_s, xp_r, 1)

            @pl.when(core == 1)
            def _():
                send_tail(2, x_r.at[2], ny)
                send_tail(3, x_r.at[2], nx)

            load(x_ref, x_all, 2)

        @pl.when(g == 3)
        def _():
            relay(x_all, x_s, x_r, xp_r, 2, False)
            from_partner(x_all, x_s, xp_r, 2)
            load(x_ref, x_all, 4)

        def weight(j, carry):
            s = pl.ds(pl.multiple_of(j * 512, 512), 512)
            d = dgu[pl.ds(pl.multiple_of(g * B, B), B), :]
            acc[s, :] += lax.dot_general(tok[slot, :, s], d, TN, preferred_element_type=F32)
            return carry

        lax.fori_loop(0, 4, weight, 0)

        @pl.when(g == 5)
        def _():
            for kind in range(2):
                both_r(kind).wait_recv()
                pltpu.make_async_copy(rs_in.at[kind], tok.at[kind], t_sem.at[kind]).start()
            both_r(0).wait_send()
            loaded(0)

            def add(i, carry):
                r = pl.ds(pl.multiple_of(i * 32, 32), 32)
                own[r, :] += tok[0, r, :].astype(F32)
                return carry

            lax.fori_loop(0, B // 32, add, 0)
            loaded(1)
            for k, dev in enumerate((nx, ny)):
                def late(j, carry):
                    s = pl.ds(pl.multiple_of(j * 512, 512), 512)
                    total = dx_tile(4 + k, H, j) + p_in[2 + k, :, s].astype(F32) + tok[1, k * H:(k + 1) * H, s].astype(F32)
                    rs_out[k, :, s] = total.astype(BF16)
                    return carry

                lax.fori_loop(0, 4, late, 0)
                send_last(k, dev).start()

            for c, n, m in ((0, H - SHIFT, 2 * H + 2 * SHIFT), (1, H, 2 * H - 2 * SHIFT)):
                @pl.when(core == c)
                def _():
                    of_rows(x_all, 4 * H - m, x_s.at[0], x_r.at[2]).wait_recv()
                    send_on(x_all, x_s, xp_r.at[3], 6, n, partner)
                    send_on(x_all, x_s, xp_r.at[3], 7, n, partner)
                    if c == 1:
                        send_tail(6, xp_r.at[3], partner)
                        send_tail(7, xp_r.at[3], partner)
                    of_rows(x_all, m, x_s.at[0], xp_r.at[3]).wait_recv()

            load(x_ref, x_all, 6)

        return carry

    lax.fori_loop(0, 8, second_pass, 0)

    def weight_out(i, carry):
        r = pl.ds(pl.multiple_of(i * 32, 32), 32)
        dwg_ref[r, :] = acc[r, 0:F].astype(BF16)
        dwu_ref[r, :] = acc[r, F:2 * F].astype(BF16)
        return carry

    lax.fori_loop(0, D // 32, weight_out, 0)

    both_r(1).wait_send()
    for g in (6, 7):
        send_p(g).wait_send()
    of_rows(dy_all, 14 * H, dy_s.at[0], dy_r.at[0]).wait_send()
    for c, m in ((0, 14 * H - 4 * SHIFT), (1, 14 * H + 4 * SHIFT)):
        @pl.when(core == c)
        def _():
            of_rows(x_all, m, x_s.at[0], x_r.at[0]).wait_send()

    ends = remote(last, last, l_s.at[0], l_r.at[0], nx)
    ends.wait_send()
    ends.wait_recv()


def finish(own, last, dwg, dwu, dwd, dx_ref, dwg_ref, dwu_ref, dwd_ref, dx, sem, dx_sem):
    copies = [
        pltpu.make_async_copy(src, dst, sem.at[i])
        for i, (src, dst) in enumerate(((dwd, dwd_ref), (dwg, dwg_ref), (dwu, dwu_ref)))
    ]
    for c in copies:
        c.start()
    for q in range(B // LAST):
        k, i = 1 - q * LAST // H, q * LAST % H

        def add(n, carry):
            r = pl.ds(pl.multiple_of(q * LAST + n * 32, 32), 32)
            dx[r, :] = (own[r, :] + last[k, pl.ds(pl.multiple_of(i + n * 32, 32), 32), :].astype(F32)).astype(BF16)
            return carry

        lax.fori_loop(0, LAST // 32, add, 0)
        r = pl.ds(q * LAST, LAST)
        copies.append(pltpu.make_async_copy(dx.at[r], dx_ref.at[r], dx_sem.at[q]))
        copies[-1].start()
    for c in copies:
        c.wait()


def solution(mesh):
    def local(*args):
        any_ = pl.BlockSpec(memory_space=pl.ANY)
        dma = pltpu.SemaphoreType.DMA
        vmem = pl.BlockSpec(memory_space=pltpu.VMEM)
        grads = [(D, F), (D, F), (F, D)]
        kept = pl.pallas_call(
            kernel,
            out_shape=[pltpu.VMEM((B, D), F32), pltpu.VMEM((2, H, D), BF16)]
            + [pltpu.VMEM(s, BF16) for s in grads]
            + [jax.ShapeDtypeStruct(s, BF16) for s in ((8 * B, D), (8 * B, D), (2, B, D))],
            in_specs=[any_] * 7,
            out_specs=[vmem] * 5 + [any_] * 3,
            scratch_shapes=[
                pltpu.VMEM((F, D), BF16),
                pltpu.VMEM((D, 2 * F), BF16),
                pltpu.VMEM((8 * B, 2 * F), BF16),
                pltpu.VMEM((D, 2 * F), F32),
                pltpu.VMEM((2, B, D), BF16),
                pltpu.VMEM((2, B, F), BF16),
                pltpu.VMEM((B, F), F32),
                pltpu.VMEM((B, F), BF16),
                pltpu.VMEM((4, H, D), BF16),
                pltpu.VMEM((2, H, D), BF16),
                pltpu.VMEM((4, H, D), BF16),
            ]
            + [dma((n,)) for n in (1, 3, 4, 1, 3, 4, 2, 2, 2, 2, 1, 1, 2, 2, 1)],
            compiler_params=pltpu.CompilerParams(collective_id=0, has_side_effects=True, vmem_limit_bytes=50 * 2**20),
            name="backward",
        )(*args)
        return tuple(
            pl.pallas_call(
                finish,
                out_shape=[jax.ShapeDtypeStruct(s, BF16) for s in [(B, D), *grads]],
                in_specs=[vmem] * 5,
                out_specs=[any_] * 4,
                scratch_shapes=[pltpu.VMEM((B, D), BF16), dma((3,)), dma((B // LAST,))],
                compiler_params=pltpu.CompilerParams(vmem_limit_bytes=24 * 2**20),
                name="finish",
            )(*kept[:5])
        )

    rows, cols = P(("dp", "tp"), None), P("dp", "tp")
    return jax.shard_map(
        local,
        mesh=mesh,
        in_specs=(rows, rows, cols, cols, P(None, "tp"), P(None, "tp"), P("tp", None)),
        out_specs=(rows, cols, cols, rows),
        check_vma=False,
    )
```

time: 214 us -> 211 us (0.986); the launches traced: 211 us -> 211 us
  no operation moved by 1% of the time
where the time goes in v5:
time: 211 us
  Pallas kernels  211 us (100%)
    pallas_call x1, Pallas kernels, local(): pl.pallas_call(kernel, out_shape=[pltpu.VMEM((B, D), F32), pltpu.VMEM((2,...  207 us

profile of v5, /device:TPU:1, one launch (start us, length us, event | category | flops | bytes accessed | tf_op | source)
XLA Modules:
  0.0 211.3 jit_solution(5191831085082506415)
XLA Ops:
  0.6 206.8 %backward.1 = (f32[512,2048]{1,0:T(8,128)S(1)}, bf16[2,256,2048]{2,1,0:T(8,128)(2,1)S(1)}, bf16[2048,640]{1,0:T(8,128)(2,1)S(1)}, bf16[2048,640]{1,0:T(8,128)(2,...) custom-call(bf16[512,2048]{1,0:T(8,128)(2,1)} %x_ref.1, ...), custom_call_target="tpu_custom_call" | custom-call | tf_op jit(solution)/shard_map/backward/pallas_call | solution.py:369
  207.4 3.8 %finish.1 = (bf16[512,2048]{1,0:T(8,128)(2,1)}, bf16[2048,640]{1,0:T(8,128)(2,1)}, bf16[2048,640]{1,0:T(8,128)(2,1)}, bf16[640,2048]{1,0:T(8,128)(2,1)}) custom-call(f32[512,2048]{1,0:T(8,128)S(1)} %get-tuple-element.9.own, bf16[2,256,2048]{2,1,0:T(8,128)(2,1)S(1)} %get-tuple-element.10.last, bf16[2048,640]{1,0:T(8,128)(2,1)S(1)} %get-tuple-element.11.dwg, ...), custom_call_target="tpu_custom_call" | custom-call | tf_op jit(solution)/shard_map/finish/pallas_call | solution.py:394

commit v6 on v5

--- a/solution.py
+++ b/solution.py
@@ -12,7 +12,7 @@
 B = 512
 H = 256
 LAST = 128
-SHIFT = 32
+SHIFT = 24
 F32 = jnp.float32
 BF16 = jnp.bfloat16
 NT = (((1,), (1,)), ((), ()))
@@ -25,7 +25,7 @@
     x_ref, dy_ref, gate_ref, up_ref, wg_ref, wu_ref, wd_ref,
     own, last, dwg_ref, dwu_ref, dwd_ref, dy_all, x_all, rs_in,
     wd, wgu, dgu, acc, tok, guv, dh, hid, p_in, p_out, rs_out,
-    dy_s, dy_r, dyp_r, x_s, x_r, xp_r, p_s, p_r, r_s, r_r, l_s, l_r, w_sem, t_sem, g_sem,
+    dy_s, dy_r, dyp_r, x_s, x_r, xp_r, p_s, p_r, r_s, r_r, l_s, l_r, w_sem, t_sem, g_sem, go,
 ):
     me = lax.axis_index("tp")
     core, iy, ix = me % 2, (me // 2) % 2, me // 4
@@ -35,10 +35,24 @@
     nx = me + 4 - 8 * ix
     nd = ny + 4 - 8 * ix
 
+    place = ix + iy
     barrier = pltpu.get_barrier_semaphore()
-    for d in (partner, nx, ny):
-        pl.semaphore_signal(barrier, inc=1, device_id={"tp": d}, device_id_type=pl.DeviceIdType.MESH)
-    pl.semaphore_wait(barrier, 3)
+
+    def signal(sem, devs):
+        for d in devs:
+            pl.semaphore_signal(sem, inc=1, device_id={"tp": d}, device_id_type=pl.DeviceIdType.MESH)
+
+    signal(barrier, (partner,))
+
+    @pl.when(place < 2)
+    def _():
+        signal(barrier, (nx, ny))
+
+    pl.semaphore_wait(barrier, jnp.where(place == 1, 2, 3))
+
+    @pl.when(place == 2)
+    def _():
+        signal(go, (nx, ny))
 
     def owner(g):
         return jnp.where(g < 2, me, jnp.where(g >= 6, nd, jnp.where(g % 2 == 0, nx, ny)))
@@ -57,9 +71,12 @@
     def of_rows(full, n, ss, rs):
         return remote(full.at[pl.ds(0, n)], full.at[pl.ds(0, n)], ss, rs, partner)
 
-    def start_own(ref, full, s, r, pr):
-        for h, p, dev in ((0, 0, nx), (1, 0, ny), (0, None, partner), (1, 1, nx), (0, 1, ny), (1, None, partner)):
-            remote(ref.at[pl.ds(h * H, H)], full.at[rows(me, h)], s.at[0], pr.at[0] if p is None else r.at[p], dev).start()
+    def start_own(ref, full, s, r, pr, to="xyp"):
+        for n in range(2):
+            for t in to:
+                h = 1 - n if t == "y" else n
+                sem, dev = {"x": (r.at[n], nx), "y": (r.at[n], ny), "p": (pr.at[0], partner)}[t]
+                remote(ref.at[pl.ds(h * H, H)], full.at[rows(me, h)], s.at[0], sem, dev).start()
 
     def send_on(full, s, r, g, n, dev):
         q = rows(owner(g), half(g), n)
@@ -98,7 +115,17 @@
             pltpu.make_async_copy(src.at[rows(o + other, h)], guv.at[i, pl.ds(0, H)], g_sem.at[0]).start()
             pltpu.make_async_copy(src.at[rows(o, h)], guv.at[i, pl.ds(H, H)], g_sem.at[0]).start()
 
-    start_own(dy_ref, dy_all, dy_s, dy_r, dyp_r)
+    @pl.when(place != 1)
+    def _():
+        start_own(dy_ref, dy_all, dy_s, dy_r, dyp_r)
+
+    for i, first, then in ((1, "xp", "y"), (0, "yp", "x")):
+        @pl.when(jnp.logical_and(place == 1, ix == i))
+        def _():
+            start_own(dy_ref, dy_all, dy_s, dy_r, dyp_r, first)
+            pl.semaphore_wait(go, 1)
+            start_own(dy_ref, dy_all, dy_s, dy_r, dyp_r, then)
+
     pltpu.make_async_copy(wd_ref, wd, w_sem.at[0]).start()
     load_gates(0)
     pltpu.make_async_copy(wg_ref, wgu.at[:, pl.ds(0, F)], w_sem.at[1]).start()
@@ -386,7 +413,8 @@
                 pltpu.VMEM((2, H, D), BF16),
                 pltpu.VMEM((4, H, D), BF16),
             ]
-            + [dma((n,)) for n in (1, 3, 4, 1, 3, 4, 2, 2, 2, 2, 1, 1, 2, 2, 1)],
+            + [dma((n,)) for n in (1, 3, 4, 1, 3, 4, 2, 2, 2, 2, 1, 1, 2, 2, 1)]
+            + [pltpu.SemaphoreType.REGULAR],
             compiler_params=pltpu.CompilerParams(collective_id=0, has_side_effects=True, vmem_limit_bytes=50 * 2**20),
             name="backward",
         )(*args)

time: 211 us -> 211 us (level)
  no operation moved by 1% of the time
where the time goes in v6:
time: 211 us
  Pallas kernels  210 us (100%)
    pallas_call x1, Pallas kernels, local(): pl.pallas_call(kernel, out_shape=[pltpu.VMEM((B, D), F32), pltpu.VMEM((2,...  206 us

profile of v6, /device:TPU:1, one launch (start us, length us, event | category | flops | bytes accessed | tf_op | source)
XLA Modules:
  0.0 210.7 jit_solution(14433328886868157672)
XLA Ops:
  0.6 206.2 %backward.1 = (f32[512,2048]{1,0:T(8,128)S(1)}, bf16[2,256,2048]{2,1,0:T(8,128)(2,1)S(1)}, bf16[2048,640]{1,0:T(8,128)(2,1)S(1)}, bf16[2048,640]{1,0:T(8,128)(2,...) custom-call(bf16[512,2048]{1,0:T(8,128)(2,1)} %x_ref.1, ...), custom_call_target="tpu_custom_call" | custom-call | tf_op jit(solution)/shard_map/backward/pallas_call | solution.py:396
  206.9 3.8 %finish.1 = (bf16[512,2048]{1,0:T(8,128)(2,1)}, bf16[2048,640]{1,0:T(8,128)(2,1)}, bf16[2048,640]{1,0:T(8,128)(2,1)}, bf16[640,2048]{1,0:T(8,128)(2,1)}) custom-call(f32[512,2048]{1,0:T(8,128)S(1)} %get-tuple-element.9.own, bf16[2,256,2048]{2,1,0:T(8,128)(2,1)S(1)} %get-tuple-element.10.last, bf16[2048,640]{1,0:T(8,128)(2,1)S(1)} %get-tuple-element.11.dwg, ...), custom_call_target="tpu_custom_call" | custom-call | tf_op jit(solution)/shard_map/finish/pallas_call | solution.py:422

commit v7 on v6

--- a/solution.py
+++ b/solution.py
@@ -25,7 +25,7 @@
     x_ref, dy_ref, gate_ref, up_ref, wg_ref, wu_ref, wd_ref,
     own, last, dwg_ref, dwu_ref, dwd_ref, dy_all, x_all, rs_in,
     wd, wgu, dgu, acc, tok, guv, dh, hid, p_in, p_out, rs_out,
-    dy_s, dy_r, dyp_r, x_s, x_r, xp_r, p_s, p_r, r_s, r_r, l_s, l_r, w_sem, t_sem, g_sem, go,
+    dy_s, dy_r, dyp_r, x_s, x_r, xp_r, p_s, p_r, r_s, r_r, l_s, l_r, w_sem, t_sem, g_sem, go_chip, go_core,
 ):
     me = lax.axis_index("tp")
     core, iy, ix = me % 2, (me // 2) % 2, me // 4
@@ -42,17 +42,23 @@
         for d in devs:
             pl.semaphore_signal(sem, inc=1, device_id={"tp": d}, device_id_type=pl.DeviceIdType.MESH)
 
-    signal(barrier, (partner,))
-
     @pl.when(place < 2)
     def _():
         signal(barrier, (nx, ny))
 
-    pl.semaphore_wait(barrier, jnp.where(place == 1, 2, 3))
+    @pl.when(core == 1)
+    def _():
+        signal(barrier, (partner,))
+
+    pl.semaphore_wait(barrier, jnp.where(place == 1, 1, 2) + 1 - core)
+
+    @pl.when(core == 0)
+    def _():
+        signal(go_core, (partner,))
 
     @pl.when(place == 2)
     def _():
-        signal(go, (nx, ny))
+        signal(go_chip, (nx, ny))
 
     def owner(g):
         return jnp.where(g < 2, me, jnp.where(g >= 6, nd, jnp.where(g % 2 == 0, nx, ny)))
@@ -115,16 +121,32 @@
             pltpu.make_async_copy(src.at[rows(o + other, h)], guv.at[i, pl.ds(0, H)], g_sem.at[0]).start()
             pltpu.make_async_copy(src.at[rows(o, h)], guv.at[i, pl.ds(H, H)], g_sem.at[0]).start()
 
+    def start_dy(to):
+        start_own(dy_ref, dy_all, dy_s, dy_r, dyp_r, to)
+
     @pl.when(place != 1)
     def _():
-        start_own(dy_ref, dy_all, dy_s, dy_r, dyp_r)
-
-    for i, first, then in ((1, "xp", "y"), (0, "yp", "x")):
+        start_dy("xy")
+
+    for i, first in ((1, "x"), (0, "y")):
         @pl.when(jnp.logical_and(place == 1, ix == i))
         def _():
-            start_own(dy_ref, dy_all, dy_s, dy_r, dyp_r, first)
-            pl.semaphore_wait(go, 1)
-            start_own(dy_ref, dy_all, dy_s, dy_r, dyp_r, then)
+            start_dy(first)
+
+    @pl.when(core == 1)
+    def _():
+        pl.semaphore_wait(go_core, 1)
+
+    start_dy("p")
+
+    @pl.when(place == 1)
+    def _():
+        pl.semaphore_wait(go_chip, 1)
+
+    for i, then in ((1, "y"), (0, "x")):
+        @pl.when(jnp.logical_and(place == 1, ix == i))
+        def _():
+            start_dy(then)
 
     pltpu.make_async_copy(wd_ref, wd, w_sem.at[0]).start()
     load_gates(0)
@@ -414,7 +436,7 @@
                 pltpu.VMEM((4, H, D), BF16),
             ]
             + [dma((n,)) for n in (1, 3, 4, 1, 3, 4, 2, 2, 2, 2, 1, 1, 2, 2, 1)]
-            + [pltpu.SemaphoreType.REGULAR],
+            + [pltpu.SemaphoreType.REGULAR] * 2,
             compiler_params=pltpu.CompilerParams(collective_id=0, has_side_effects=True, vmem_limit_bytes=50 * 2**20),
             name="backward",
         )(*args)

time: 211 us -> 210 us (level)
  no operation moved by 1% of the time
where the time goes in v7:
time: 210 us
  Pallas kernels  210 us (100%)
    pallas_call x1, Pallas kernels, local(): pl.pallas_call(kernel, out_shape=[pltpu.VMEM((B, D), F32), pltpu.VMEM((2,...  206 us

profile of v7, /device:TPU:1, one launch (start us, length us, event | category | flops | bytes accessed | tf_op | source)
XLA Modules:
  0.0 210.2 jit_solution(444941564063744182)
XLA Ops:
  0.6 205.7 %backward.1 = (f32[512,2048]{1,0:T(8,128)S(1)}, bf16[2,256,2048]{2,1,0:T(8,128)(2,1)S(1)}, bf16[2048,640]{1,0:T(8,128)(2,1)S(1)}, bf16[2048,640]{1,0:T(8,128)(2,...) custom-call(bf16[512,2048]{1,0:T(8,128)(2,1)} %x_ref.1, ...), custom_call_target="tpu_custom_call" | custom-call | tf_op jit(solution)/shard_map/backward/pallas_call | solution.py:418
  206.3 3.8 %finish.1 = (bf16[512,2048]{1,0:T(8,128)(2,1)}, bf16[2048,640]{1,0:T(8,128)(2,1)}, bf16[2048,640]{1,0:T(8,128)(2,1)}, bf16[640,2048]{1,0:T(8,128)(2,1)}) custom-call(f32[512,2048]{1,0:T(8,128)S(1)} %get-tuple-element.9.own, bf16[2,256,2048]{2,1,0:T(8,128)(2,1)S(1)} %get-tuple-element.10.last, bf16[2048,640]{1,0:T(8,128)(2,1)S(1)} %get-tuple-element.11.dwg, ...), custom_call_target="tpu_custom_call" | custom-call | tf_op jit(solution)/shard_map/finish/pallas_call | solution.py:444

commit v8 on v7

--- a/solution.py
+++ b/solution.py
@@ -12,7 +12,7 @@
 B = 512
 H = 256
 LAST = 128
-SHIFT = 24
+RS = ((2, 1, 1, 0), (3, 1, 0, 1), (0, 0, 0, 0), (1, 0, 1, 1))
 F32 = jnp.float32
 BF16 = jnp.bfloat16
 NT = (((1,), (1,)), ((), ()))
@@ -23,9 +23,9 @@
 
 def kernel(
     x_ref, dy_ref, gate_ref, up_ref, wg_ref, wu_ref, wd_ref,
-    own, last, dwg_ref, dwu_ref, dwd_ref, dy_all, x_all, rs_in,
-    wd, wgu, dgu, acc, tok, guv, dh, hid, p_in, p_out, rs_out,
-    dy_s, dy_r, dyp_r, x_s, x_r, xp_r, p_s, p_r, r_s, r_r, l_s, l_r, w_sem, t_sem, g_sem, go_chip, go_core,
+    sums, rs_out, dwg_ref, dwu_ref, dwd_ref, dy_all, x_all, rs_in,
+    wd, wgu, dgu, acc, tok, guv, dh, hid, p_in, p_out,
+    dy_s, dy_r, dyp_r, x_s, x_r, xp_r, p_s, p_r, r_s, r_r, w_sem, t_sem, g_sem, go_chip, go_core,
 ):
     me = lax.axis_index("tp")
     core, iy, ix = me % 2, (me // 2) % 2, me // 4
@@ -158,20 +158,14 @@
     pltpu.make_async_copy(wd_ref, wd, w_sem.at[0]).wait()
     pltpu.make_async_copy(wgu, wgu, w_sem.at[1]).wait()
 
-    def p_slot(g):
-        return jnp.where(jnp.logical_or(g == 4, g == 5), g - 2, g % 2)
-
     def send_p(g):
-        return remote(p_out.at[g % 2], p_in.at[p_slot(g)], p_s.at[g % 2], p_r.at[g % 2], partner)
+        return remote(p_out.at[g % 2], p_in.at[g % 2], p_s.at[g % 2], p_r.at[g % 2], partner)
 
     def send_r(stage, kind, k, dev):
-        return remote(rs_out.at[stage], rs_in.at[kind, pl.ds(k * H, H)], r_s.at[kind], r_r.at[kind], dev)
+        return remote(rs_out.at[stage], rs_in.at[kind, k], r_s.at[kind], r_r.at[kind], dev)
 
     def both_r(kind):
         return remote(rs_in.at[kind], rs_in.at[kind], r_s.at[kind], r_r.at[kind], nx)
-
-    def send_last(k, dev):
-        return remote(rs_out.at[k], last.at[k], l_s.at[0], l_r.at[0], dev)
 
     def dx_tile(g, r0, j):
         a = dgu[pl.ds(pl.multiple_of(g * B + r0, H), H), :]
@@ -245,43 +239,36 @@
 
         send_p(g).wait_recv()
 
-        @pl.when(jnp.logical_or(g < 4, g >= 6))
-        def _():
-            def m_rows(j, carry):
-                s = pl.ds(pl.multiple_of(j * 512, 512), 512)
-                total = dx_tile(g, H, j) + p_in[p_slot(g), :, s].astype(F32)
-
-                @pl.when(g < 2)
-                def _():
-                    own[pl.ds(pl.multiple_of(slot * H, H), H), s] = total
-
-                @pl.when(g >= 2)
-                def _():
-                    rs_out[jnp.where(g >= 6, g - 4, slot), :, s] = total.astype(BF16)
-
-                return carry
-
-            lax.fori_loop(0, 4, m_rows, 0)
-
-        for group, stage, kind, k, dev in ((2, 0, 0, 0, nx), (3, 1, 0, 1, ny), (6, 2, 1, 1, nx), (7, 3, 1, 0, ny)):
-            @pl.when(g == group)
+        def m_rows(j, carry):
+            s = pl.ds(pl.multiple_of(j * 512, 512), 512)
+            total = dx_tile(g, H, j) + p_in[slot, :, s].astype(F32)
+
+            @pl.when(g // 2 % 2 == 0)
             def _():
-                send_r(stage, kind, k, dev).start()
-
+                sums[g // 2 + slot, :, s] = total
+
+            @pl.when(g // 2 % 2 == 1)
+            def _():
+                rs_out[jnp.where(g >= 6, g - 4, slot), :, s] = total.astype(BF16)
+
+            return carry
+
+        lax.fori_loop(0, 4, m_rows, 0)
         return carry
 
     lax.fori_loop(0, 8, first_pass, 0)
+
+    relay(x_all, x_s, x_r, xp_r, 1, True)
+
+    @pl.when(core == 0)
+    def _():
+        for stage, kind, k, dev in RS:
+            send_r(stage, kind, k, (nx, ny)[dev]).start()
 
     for j in range(4):
         dwd_ref[:, j * 512:j * 512 + 512] = acc[j // 2 * F:j // 2 * F + F, j % 2 * 512:j % 2 * 512 + 512].astype(BF16)
     acc[...] = jnp.zeros_like(acc)
 
-    def tail(g):
-        return pl.ds(pl.multiple_of((owner(g) - core) * B + half(g) * H + H - SHIFT, 8), SHIFT)
-
-    def send_tail(g, r, dev):
-        remote(x_all.at[tail(g)], x_all.at[tail(g)], x_s.at[0], r, dev).start()
-
     def second_pass(g, carry):
         slot = g % 2
         loaded(slot)
@@ -292,20 +279,7 @@
 
         @pl.when(g == 1)
         def _():
-            relay(x_all, x_s, x_r, xp_r, 1, False)
-            for c, n in ((0, H - SHIFT), (1, H)):
-                @pl.when(core == c)
-                def _():
-                    send_on(x_all, x_s, x_r.at[2], 2, n, ny)
-                    send_on(x_all, x_s, x_r.at[2], 3, n, nx)
-
             from_partner(x_all, x_s, xp_r, 1)
-
-            @pl.when(core == 1)
-            def _():
-                send_tail(2, x_r.at[2], ny)
-                send_tail(3, x_r.at[2], nx)
-
             load(x_ref, x_all, 2)
 
         @pl.when(g == 3)
@@ -324,40 +298,8 @@
 
         @pl.when(g == 5)
         def _():
-            for kind in range(2):
-                both_r(kind).wait_recv()
-                pltpu.make_async_copy(rs_in.at[kind], tok.at[kind], t_sem.at[kind]).start()
-            both_r(0).wait_send()
-            loaded(0)
-
-            def add(i, carry):
-                r = pl.ds(pl.multiple_of(i * 32, 32), 32)
-                own[r, :] += tok[0, r, :].astype(F32)
-                return carry
-
-            lax.fori_loop(0, B // 32, add, 0)
-            loaded(1)
-            for k, dev in enumerate((nx, ny)):
-                def late(j, carry):
-                    s = pl.ds(pl.multiple_of(j * 512, 512), 512)
-                    total = dx_tile(4 + k, H, j) + p_in[2 + k, :, s].astype(F32) + tok[1, k * H:(k + 1) * H, s].astype(F32)
-                    rs_out[k, :, s] = total.astype(BF16)
-                    return carry
-
-                lax.fori_loop(0, 4, late, 0)
-                send_last(k, dev).start()
-
-            for c, n, m in ((0, H - SHIFT, 2 * H + 2 * SHIFT), (1, H, 2 * H - 2 * SHIFT)):
-                @pl.when(core == c)
-                def _():
-                    of_rows(x_all, 4 * H - m, x_s.at[0], x_r.at[2]).wait_recv()
-                    send_on(x_all, x_s, xp_r.at[3], 6, n, partner)
-                    send_on(x_all, x_s, xp_r.at[3], 7, n, partner)
-                    if c == 1:
-                        send_tail(6, xp_r.at[3], partner)
-                        send_tail(7, xp_r.at[3], partner)
-                    of_rows(x_all, m, x_s.at[0], xp_r.at[3]).wait_recv()
-
+            relay(x_all, x_s, x_r, xp_r, 3, False)
+            from_partner(x_all, x_s, xp_r, 3)
             load(x_ref, x_all, 6)
 
         return carry
@@ -372,38 +314,100 @@
 
     lax.fori_loop(0, D // 32, weight_out, 0)
 
-    both_r(1).wait_send()
     for g in (6, 7):
         send_p(g).wait_send()
     of_rows(dy_all, 14 * H, dy_s.at[0], dy_r.at[0]).wait_send()
-    for c, m in ((0, 14 * H - 4 * SHIFT), (1, 14 * H + 4 * SHIFT)):
-        @pl.when(core == c)
-        def _():
-            of_rows(x_all, m, x_s.at[0], x_r.at[0]).wait_send()
-
-    ends = remote(last, last, l_s.at[0], l_r.at[0], nx)
-    ends.wait_send()
-    ends.wait_recv()
-
-
-def finish(own, last, dwg, dwu, dwd, dx_ref, dwg_ref, dwu_ref, dwd_ref, dx, sem, dx_sem):
+    of_rows(x_all, 14 * H, x_s.at[0], x_r.at[0]).wait_send()
+
+    @pl.when(core == 0)
+    def _():
+        for kind in range(2):
+            both_r(kind).wait_send()
+            both_r(kind).wait_recv()
+
+
+def write_dw(dwg, dwu, dwd, dwg_ref, dwu_ref, dwd_ref, done, sem):
     copies = [
         pltpu.make_async_copy(src, dst, sem.at[i])
         for i, (src, dst) in enumerate(((dwd, dwd_ref), (dwg, dwg_ref), (dwu, dwu_ref)))
     ]
     for c in copies:
         c.start()
+    done[...] = jnp.zeros_like(done)
+    for c in copies:
+        c.wait()
+
+
+def exchange(sums, rs_out, rs_in, done, got, diag, stage, s_sem, r_sem, t_sem):
+    del done
+    me = lax.axis_index("tp")
+    core, iy, ix = me % 2, (me // 2) % 2, me // 4
+    near = (me + 4 - 8 * ix, me + 2 - 4 * iy)
+
+    barrier = pltpu.get_barrier_semaphore()
+    for d in near:
+        pl.semaphore_signal(barrier, inc=1, device_id={"tp": d}, device_id_type=pl.DeviceIdType.MESH)
+    pl.semaphore_wait(barrier, 2)
+
+    def remote(src, dst, i, dev):
+        return pltpu.make_async_remote_copy(
+            src_ref=src, dst_ref=dst, send_sem=s_sem.at[i], recv_sem=r_sem.at[i],
+            device_id={"tp": dev}, device_id_type=pl.DeviceIdType.MESH,
+        )
+
+    firsts, diags = got.at[pl.ds(0, 2)], remote(diag, diag, 1, near[0])
+    local = [
+        pltpu.make_async_copy(rs_in.at[1], diag, t_sem.at[1]),
+        pltpu.make_async_copy(rs_in.at[0], firsts, t_sem.at[0]),
+    ]
+
+    @pl.when(core == 1)
+    def _():
+        for st, kind, k, dev in RS:
+            remote(rs_out.at[st], (firsts, diag)[kind].at[k], kind, near[dev]).start()
+        diags.wait_recv()
+
+    @pl.when(core == 0)
+    def _():
+        for c in local:
+            c.start()
+        local[0].wait()
+
+    for k in range(2):
+        def add(i, carry):
+            r = pl.ds(pl.multiple_of(i * 32, 32), 32)
+            stage[k, r, :] = (sums[2 + k, r, :] + diag[k, r, :].astype(F32)).astype(BF16)
+            return carry
+
+        lax.fori_loop(0, H // 32, add, 0)
+        remote(stage.at[k], got.at[2 + k], 2, near[k]).start()
+
+    @pl.when(core == 1)
+    def _():
+        diags.wait_send()
+        remote(firsts, firsts, 0, near[0]).wait()
+
+    @pl.when(core == 0)
+    def _():
+        local[1].wait()
+
+    remote(stage, got.at[pl.ds(2, 2)], 2, near[0]).wait()
+
+
+def write_dx(sums, got, dx_ref, dx, sem):
+    copies = []
     for q in range(B // LAST):
-        k, i = 1 - q * LAST // H, q * LAST % H
+        h, i = q * LAST // H, q * LAST % H
 
         def add(n, carry):
             r = pl.ds(pl.multiple_of(q * LAST + n * 32, 32), 32)
-            dx[r, :] = (own[r, :] + last[k, pl.ds(pl.multiple_of(i + n * 32, 32), 32), :].astype(F32)).astype(BF16)
+            p = pl.ds(pl.multiple_of(i + n * 32, 32), 32)
+            dx[r, :] = (sums[h, p, :] + got[h, p, :].astype(F32) + got[3 - h, p, :].astype(F32)).astype(BF16)
             return carry
 
         lax.fori_loop(0, LAST // 32, add, 0)
         r = pl.ds(q * LAST, LAST)
-        copies.append(pltpu.make_async_copy(dx.at[r], dx_ref.at[r], dx_sem.at[q]))
+        copies.append(pltpu.make_async_copy(dx.at[r], dx_ref.at[r], sem.at[q]))
         copies[-1].start()
     for c in copies:
         c.wait()
@@ -415,11 +419,15 @@
         dma = pltpu.SemaphoreType.DMA
         vmem = pl.BlockSpec(memory_space=pltpu.VMEM)
         grads = [(D, F), (D, F), (F, D)]
-        kept = pl.pallas_call(
+        def held(a):
+            return pltpu.with_memory_space_constraint(a, pltpu.VMEM)
+
+        hbm = [jax.ShapeDtypeStruct(s, BF16) for s in ((8 * B, D), (8 * B, D), (2, 2, H, D))]
+        sums, rs_out, *dws, _, _, rs_in = pl.pallas_call(
             kernel,
-            out_shape=[pltpu.VMEM((B, D), F32), pltpu.VMEM((2, H, D), BF16)]
+            out_shape=[pltpu.VMEM((4, H, D), F32), pltpu.VMEM((4, H, D), BF16)]
             + [pltpu.VMEM(s, BF16) for s in grads]
-            + [jax.ShapeDtypeStruct(s, BF16) for s in ((8 * B, D), (8 * B, D), (2, B, D))],
+            + hbm,
             in_specs=[any_] * 7,
             out_specs=[vmem] * 5 + [any_] * 3,
             scratch_shapes=[
@@ -431,26 +439,42 @@
                 pltpu.VMEM((2, B, F), BF16),
                 pltpu.VMEM((B, F), F32),
                 pltpu.VMEM((B, F), BF16),
-                pltpu.VMEM((4, H, D), BF16),
                 pltpu.VMEM((2, H, D), BF16),
-                pltpu.VMEM((4, H, D), BF16),
+                pltpu.VMEM((2, H, D), BF16),
             ]
-            + [dma((n,)) for n in (1, 3, 4, 1, 3, 4, 2, 2, 2, 2, 1, 1, 2, 2, 1)]
+            + [dma((n,)) for n in (1, 3, 4, 1, 3, 4, 2, 2, 2, 2, 2, 2, 1)]
             + [pltpu.SemaphoreType.REGULAR] * 2,
-            compiler_params=pltpu.CompilerParams(collective_id=0, has_side_effects=True, vmem_limit_bytes=50 * 2**20),
+            compiler_params=pltpu.CompilerParams(collective_id=0, has_side_effects=True, vmem_limit_bytes=42 * 2**20),
             name="backward",
         )(*args)
-        return tuple(
-            pl.pallas_call(
-                finish,
-                out_shape=[jax.ShapeDtypeStruct(s, BF16) for s in [(B, D), *grads]],
-                in_specs=[vmem] * 5,
-                out_specs=[any_] * 4,
-                scratch_shapes=[pltpu.VMEM((B, D), BF16), dma((3,)), dma((B // LAST,))],
-                compiler_params=pltpu.CompilerParams(vmem_limit_bytes=24 * 2**20),
-                name="finish",
-            )(*kept[:5])
-        )
+        *dws, done = pl.pallas_call(
+            write_dw,
+            out_shape=[jax.ShapeDtypeStruct(s, BF16) for s in grads] + [jax.ShapeDtypeStruct((8, 128), F32)],
+            in_specs=[vmem] * 3,
+            out_specs=[any_] * 3 + [vmem],
+            scratch_shapes=[dma((3,))],
+            compiler_params=pltpu.CompilerParams(vmem_limit_bytes=16 * 2**20),
+            name="write_dw",
+        )(*map(held, dws))
+        got = pl.pallas_call(
+            exchange,
+            out_shape=pltpu.VMEM((4, H, D), BF16),
+            in_specs=[vmem, vmem, pl.BlockSpec(memory_space=pltpu.HBM), vmem],
+            out_specs=vmem,
+            scratch_shapes=[pltpu.VMEM((2, H, D), BF16)] * 2 + [dma((3,)), dma((3,)), dma((2,))],
+            compiler_params=pltpu.CompilerParams(collective_id=1, has_side_effects=True, vmem_limit_bytes=24 * 2**20),
+            name="exchange",
+        )(held(sums), held(rs_out), pltpu.with_memory_space_constraint(rs_in, pltpu.HBM), held(done))
+        dx = pl.pallas_call(
+            write_dx,
+            out_shape=jax.ShapeDtypeStruct((B, D), BF16),
+            in_specs=[vmem] * 2,
+            out_specs=any_,
+            scratch_shapes=[pltpu.VMEM((B, D), BF16), dma((B // LAST,))],
+            compiler_params=pltpu.CompilerParams(vmem_limit_bytes=16 * 2**20),
+            name="write_dx",
+        )(held(sums), held(got))
+        return dx, *dws
 
     rows, cols = P(("dp", "tp"), None), P("dp", "tp")
     return jax.shard_map(

time: 210 us -> 208 us (level)
  Pallas kernels: 210 us -> 207 us
    pallas_call x2 -> x4, Pallas kernels: 210 us -> 207 us  [the longest x1 152 us: local(): pl.pallas_call(kernel, out_shape=[pltpu.VMEM((4, H, D), F32), pltpu.VMEM(...]
where the time goes in v8:
time: 208 us
  Pallas kernels  207 us (100%)
    pallas_call x1, Pallas kernels, local(): pl.pallas_call(kernel, out_shape=[pltpu.VMEM((4, H, D), F32), pltpu.VMEM(...  152 us
    pallas_call x1, Pallas kernels, local(): pl.pallas_call(exchange, out_shape=pltpu.VMEM((4, H, D), BF16), in_specs=...  49.7 us

profile of v8, /device:TPU:1, one launch (start us, length us, event | category | flops | bytes accessed | tf_op | source)
XLA Modules:
  0.0 207.7 jit_solution(1002557638504944427)
XLA Ops:
  0.6 152.4 %backward.1 = (f32[4,256,2048]{2,1,0:T(8,128)S(1)}, bf16[4,256,2048]{2,1,0:T(8,128)(2,1)S(1)}, bf16[2048,640]{1,0:T(8,128)(2,1)S(1)}, bf16[2048,640]{1,0:T(8,128...) custom-call(bf16[512,2048]{1,0:T(8,128)(2,1)} %x_ref.1, ...), custom_call_target="tpu_custom_call" | custom-call | tf_op jit(solution)/shard_map/backward/pallas_call | solution.py:426
  153.1 3.2 %write_dw.1 = (bf16[2048,640]{1,0:T(8,128)(2,1)}, bf16[2048,640]{1,0:T(8,128)(2,1)}, bf16[640,2048]{1,0:T(8,128)(2,1)}, f32[8,128]{1,0:T(8,128)S(1)}) custom-call(bf16[2048,640]{1,0:T(8,128)(2,1)S(1)} %get-tuple-element.17.dwg, bf16[2048,640]{1,0:T(8,128)(2,1)S(1)} %get-tuple-element.18.dwu, bf16[640,2048]{1,0:T(8,128)(2,1)S(1)} %get-tuple-element.19.dwd), custom_call_target="tpu_custom_call" | custom-call | tf_op jit(solution)/shard_map/write_dw/pallas_call | solution.py:450
  156.3 49.7 %exchange.1.got = bf16[4,256,2048]{2,1,0:T(8,128)(2,1)S(1)} custom-call(f32[4,256,2048]{2,1,0:T(8,128)S(1)} %get-tuple-element.14.sums, bf16[4,256,2048]{2,1,0:T(8,128)(2,1)S(1)} %get-tuple-element.15.rs_out, bf16[2,2,256,2048]{3,2,1,0:T(8,128)(2,1)} %get-tuple-element.16.rs_in, f32[8,128]{1,0:T(8,128)S(1)} %get-tuple-element.20.done), custom_call_target="tpu_custom_call" | custom-call | tf_op jit(solution)/shard_map/exchange/pallas_call | solution.py:459
  206.1 1.6 write_dx.1

commit v9 on v8

--- a/solution.py
+++ b/solution.py
@@ -11,7 +11,7 @@
 F = 640
 B = 512
 H = 256
-LAST = 128
+LAST = 32
 RS = ((2, 1, 1, 0), (3, 1, 0, 1), (0, 0, 0, 0), (1, 0, 1, 1))
 F32 = jnp.float32
 BF16 = jnp.bfloat16
@@ -338,7 +338,7 @@
         c.wait()
 
 
-def exchange(sums, rs_out, rs_in, done, got, diag, stage, s_sem, r_sem, t_sem):
+def exchange(sums, rs_out, rs_in, done, got, diag, stage, s_sem, r_sem):
     del done
     me = lax.axis_index("tp")
     core, iy, ix = me % 2, (me // 2) % 2, me // 4
@@ -351,14 +351,14 @@
 
     def remote(src, dst, i, dev):
         return pltpu.make_async_remote_copy(
-            src_ref=src, dst_ref=dst, send_sem=s_sem.at[i], recv_sem=r_sem.at[i],
+            src_ref=src, dst_ref=dst, send_sem=s_sem.at[0], recv_sem=r_sem.at[i],
             device_id={"tp": dev}, device_id_type=pl.DeviceIdType.MESH,
         )
 
     firsts, diags = got.at[pl.ds(0, 2)], remote(diag, diag, 1, near[0])
     local = [
-        pltpu.make_async_copy(rs_in.at[1], diag, t_sem.at[1]),
-        pltpu.make_async_copy(rs_in.at[0], firsts, t_sem.at[0]),
+        pltpu.make_async_copy(rs_in.at[1], diag, r_sem.at[1]),
+        pltpu.make_async_copy(rs_in.at[0], firsts, r_sem.at[0]),
     ]
 
     @pl.when(core == 1)
@@ -380,37 +380,25 @@
             return carry
 
         lax.fori_loop(0, H // 32, add, 0)
-        remote(stage.at[k], got.at[2 + k], 2, near[k]).start()
-
-    @pl.when(core == 1)
-    def _():
-        diags.wait_send()
-        remote(firsts, firsts, 0, near[0]).wait()
-
-    @pl.when(core == 0)
-    def _():
-        local[1].wait()
-
-    remote(stage, got.at[pl.ds(2, 2)], 2, near[0]).wait()
+        remote(stage.at[k], got.at[2 + k], 0, near[k]).start()
+
+    for c, sent in ((0, stage), (1, got)):
+        @pl.when(core == c)
+        def _():
+            remote(sent, sent, 0, near[0]).wait_send()
+            if c == 1:
+                diags.wait_send()
+
+    remote(got, got, 0, near[0]).wait_recv()
 
 
 def write_dx(sums, got, dx_ref, dx, sem):
-    copies = []
     for q in range(B // LAST):
         h, i = q * LAST // H, q * LAST % H
-
-        def add(n, carry):
-            r = pl.ds(pl.multiple_of(q * LAST + n * 32, 32), 32)
-            p = pl.ds(pl.multiple_of(i + n * 32, 32), 32)
-            dx[r, :] = (sums[h, p, :] + got[h, p, :].astype(F32) + got[3 - h, p, :].astype(F32)).astype(BF16)
-            return carry
-
-        lax.fori_loop(0, LAST // 32, add, 0)
-        r = pl.ds(q * LAST, LAST)
-        copies.append(pltpu.make_async_copy(dx.at[r], dx_ref.at[r], sem.at[q]))
-        copies[-1].start()
-    for c in copies:
-        c.wait()
+        r, p = pl.ds(q * LAST, LAST), pl.ds(i, LAST)
+        dx[r, :] = (sums[h, p, :] + got[h, p, :].astype(F32) + got[3 - h, p, :].astype(F32)).astype(BF16)
+        pltpu.make_async_copy(dx.at[r], dx_ref.at[r], sem).start()
+    pltpu.make_async_copy(dx, dx_ref, sem).wait()
 
 
 def solution(mesh):
@@ -461,7 +449,7 @@
             out_shape=pltpu.VMEM((4, H, D), BF16),
             in_specs=[vmem, vmem, pl.BlockSpec(memory_space=pltpu.HBM), vmem],
             out_specs=vmem,
-            scratch_shapes=[pltpu.VMEM((2, H, D), BF16)] * 2 + [dma((3,)), dma((3,)), dma((2,))],
+            scratch_shapes=[pltpu.VMEM((2, H, D), BF16)] * 2 + [dma((1,)), dma((2,))],
             compiler_params=pltpu.CompilerParams(collective_id=1, has_side_effects=True, vmem_limit_bytes=24 * 2**20),
             name="exchange",
         )(held(sums), held(rs_out), pltpu.with_memory_space_constraint(rs_in, pltpu.HBM), held(done))
@@ -470,7 +458,7 @@
             out_shape=jax.ShapeDtypeStruct((B, D), BF16),
             in_specs=[vmem] * 2,
             out_specs=any_,
-            scratch_shapes=[pltpu.VMEM((B, D), BF16), dma((B // LAST,))],
+            scratch_shapes=[pltpu.VMEM((B, D), BF16), dma],
             compiler_params=pltpu.CompilerParams(vmem_limit_bytes=16 * 2**20),
             name="write_dx",
         )(held(sums), held(got))

time: 208 us -> 208 us (level)
  no operation moved by 1% of the time
where the time goes in v9:
time: 208 us; the launch traced here: 207 us
  Pallas kernels  207 us (100%)
    pallas_call x1, Pallas kernels, local(): pl.pallas_call(kernel, out_shape=[pltpu.VMEM((4, H, D), F32), pltpu.VMEM(...  152 us
    pallas_call x1, Pallas kernels, local(): pl.pallas_call(exchange, out_shape=pltpu.VMEM((4, H, D), BF16), in_specs=...  49.7 us

profile of v9, /device:TPU:1, one launch (start us, length us, event | category | flops | bytes accessed | tf_op | source)
XLA Modules:
  0.0 207.4 jit_solution(3004789392600761331)
XLA Ops:
  0.6 152.4 %backward.1 = (f32[4,256,2048]{2,1,0:T(8,128)S(1)}, bf16[4,256,2048]{2,1,0:T(8,128)(2,1)S(1)}, bf16[2048,640]{1,0:T(8,128)(2,1)S(1)}, bf16[2048,640]{1,0:T(8,128...) custom-call(bf16[512,2048]{1,0:T(8,128)(2,1)} %x_ref.1, ...), custom_call_target="tpu_custom_call" | custom-call | tf_op jit(solution)/shard_map/backward/pallas_call | solution.py:414
  153.1 3.2 %write_dw.1 = (bf16[2048,640]{1,0:T(8,128)(2,1)}, bf16[2048,640]{1,0:T(8,128)(2,1)}, bf16[640,2048]{1,0:T(8,128)(2,1)}, f32[8,128]{1,0:T(8,128)S(1)}) custom-call(bf16[2048,640]{1,0:T(8,128)(2,1)S(1)} %get-tuple-element.17.dwg, bf16[2048,640]{1,0:T(8,128)(2,1)S(1)} %get-tuple-element.18.dwu, bf16[640,2048]{1,0:T(8,128)(2,1)S(1)} %get-tuple-element.19.dwd), custom_call_target="tpu_custom_call" | custom-call | tf_op jit(solution)/shard_map/write_dw/pallas_call | solution.py:438
  156.3 49.7 %exchange.1.got = bf16[4,256,2048]{2,1,0:T(8,128)(2,1)S(1)} custom-call(f32[4,256,2048]{2,1,0:T(8,128)S(1)} %get-tuple-element.14.sums, bf16[4,256,2048]{2,1,0:T(8,128)(2,1)S(1)} %get-tuple-element.15.rs_out, bf16[2,2,256,2048]{3,2,1,0:T(8,128)(2,1)} %get-tuple-element.16.rs_in, f32[8,128]{1,0:T(8,128)S(1)} %get-tuple-element.20.done), custom_call_target="tpu_custom_call" | custom-call | tf_op jit(solution)/shard_map/exchange/pallas_call | solution.py:447
  206.0 1.4 write_dx.1

commit v10 on v9

--- a/solution.py
+++ b/solution.py
@@ -11,7 +11,7 @@
 F = 640
 B = 512
 H = 256
-LAST = 32
+LAST = 16
 RS = ((2, 1, 1, 0), (3, 1, 0, 1), (0, 0, 0, 0), (1, 0, 1, 1))
 F32 = jnp.float32
 BF16 = jnp.bfloat16

time: 208 us -> 208 us (level)
  no operation moved by 1% of the time
where the time goes in v10:
time: 208 us; the launch traced here: 207 us
  Pallas kernels  207 us (100%)
    pallas_call x1, Pallas kernels, local(): pl.pallas_call(kernel, out_shape=[pltpu.VMEM((4, H, D), F32), pltpu.VMEM(...  152 us
    pallas_call x1, Pallas kernels, local(): pl.pallas_call(exchange, out_shape=pltpu.VMEM((4, H, D), BF16), in_specs=...  49.7 us

profile of v10, /device:TPU:1, one launch (start us, length us, event | category | flops | bytes accessed | tf_op | source)
XLA Modules:
  0.0 207.4 jit_solution(8707083004770169528)
XLA Ops:
  0.6 152.4 %backward.1 = (f32[4,256,2048]{2,1,0:T(8,128)S(1)}, bf16[4,256,2048]{2,1,0:T(8,128)(2,1)S(1)}, bf16[2048,640]{1,0:T(8,128)(2,1)S(1)}, bf16[2048,640]{1,0:T(8,128...) custom-call(bf16[512,2048]{1,0:T(8,128)(2,1)} %x_ref.1, ...), custom_call_target="tpu_custom_call" | custom-call | tf_op jit(solution)/shard_map/backward/pallas_call | solution.py:414
  153.1 3.2 %write_dw.1 = (bf16[2048,640]{1,0:T(8,128)(2,1)}, bf16[2048,640]{1,0:T(8,128)(2,1)}, bf16[640,2048]{1,0:T(8,128)(2,1)}, f32[8,128]{1,0:T(8,128)S(1)}) custom-call(bf16[2048,640]{1,0:T(8,128)(2,1)S(1)} %get-tuple-element.17.dwg, bf16[2048,640]{1,0:T(8,128)(2,1)S(1)} %get-tuple-element.18.dwu, bf16[640,2048]{1,0:T(8,128)(2,1)S(1)} %get-tuple-element.19.dwd), custom_call_target="tpu_custom_call" | custom-call | tf_op jit(solution)/shard_map/write_dw/pallas_call | solution.py:438
  156.3 49.7 %exchange.1.got = bf16[4,256,2048]{2,1,0:T(8,128)(2,1)S(1)} custom-call(f32[4,256,2048]{2,1,0:T(8,128)S(1)} %get-tuple-element.14.sums, bf16[4,256,2048]{2,1,0:T(8,128)(2,1)S(1)} %get-tuple-element.15.rs_out, bf16[2,2,256,2048]{3,2,1,0:T(8,128)(2,1)} %get-tuple-element.16.rs_in, f32[8,128]{1,0:T(8,128)S(1)} %get-tuple-element.20.done), custom_call_target="tpu_custom_call" | custom-call | tf_op jit(solution)/shard_map/exchange/pallas_call | solution.py:447
  206.0 1.3 write_dx.1

commit v11 on v10

--- a/solution.py
+++ b/solution.py
@@ -99,9 +99,12 @@
     def from_partner(full, s, pr, p):
         of_rows(full, 2 * H, s.at[0], pr.at[p]).wait_recv()
 
-    def load(ref, full, g):
+    def load_theirs(full, g):
+        src = full.at[rows(owner(g) + other, half(g))]
+        pltpu.make_async_copy(src, tok.at[g % 2, pl.ds(0, H)], t_sem.at[g % 2]).start()
+
+    def load_mine(ref, full, g):
         o, h, slot = owner(g), half(g), g % 2
-        pltpu.make_async_copy(full.at[rows(o + other, h)], tok.at[slot, pl.ds(0, H)], t_sem.at[slot]).start()
 
         @pl.when(g < 2)
         def _():
@@ -111,6 +114,10 @@
         @pl.when(g >= 2)
         def _():
             pltpu.make_async_copy(full.at[rows(o, h)], tok.at[slot, pl.ds(H, H)], t_sem.at[slot]).start()
+
+    def load(ref, full, g):
+        load_theirs(full, g)
+        load_mine(ref, full, g)
 
     def loaded(slot):
         pltpu.make_async_copy(dy_all.at[pl.ds(0, B)], tok.at[slot], t_sem.at[slot]).wait()
@@ -152,8 +159,9 @@
     load_gates(0)
     pltpu.make_async_copy(wg_ref, wgu.at[:, pl.ds(0, F)], w_sem.at[1]).start()
     pltpu.make_async_copy(wu_ref, wgu.at[:, pl.ds(F, F)], w_sem.at[1]).start()
+    load_mine(dy_ref, dy_all, 0)
     from_partner(dy_all, dy_s, dyp_r, 0)
-    load(dy_ref, dy_all, 0)
+    load_theirs(dy_all, 0)
     acc[...] = jnp.zeros_like(acc)
     pltpu.make_async_copy(wd_ref, wd, w_sem.at[0]).wait()
     pltpu.make_async_copy(wgu, wgu, w_sem.at[1]).wait()
@@ -299,8 +307,9 @@
         @pl.when(g == 5)
         def _():
             relay(x_all, x_s, x_r, xp_r, 3, False)
+            load_mine(x_ref, x_all, 6)
             from_partner(x_all, x_s, xp_r, 3)
-            load(x_ref, x_all, 6)
+            load_theirs(x_all, 6)
 
         return carry
 

time: 208 us -> 208 us (level)
  no operation moved by 1% of the time
where the time goes in v11:
time: 208 us; the launch traced here: 207 us
  Pallas kernels  207 us (100%)
    pallas_call x1, Pallas kernels, local(): pl.pallas_call(kernel, out_shape=[pltpu.VMEM((4, H, D), F32), pltpu.VMEM(...  152 us
    pallas_call x1, Pallas kernels, local(): pl.pallas_call(exchange, out_shape=pltpu.VMEM((4, H, D), BF16), in_specs=...  50 us

profile of v11, /device:TPU:1, one launch (start us, length us, event | category | flops | bytes accessed | tf_op | source)
XLA Modules:
  0.0 207.4 jit_solution(13122802239897701928)
XLA Ops:
  0.6 152.1 %backward.1 = (f32[4,256,2048]{2,1,0:T(8,128)S(1)}, bf16[4,256,2048]{2,1,0:T(8,128)(2,1)S(1)}, bf16[2048,640]{1,0:T(8,128)(2,1)S(1)}, bf16[2048,640]{1,0:T(8,128...) custom-call(bf16[512,2048]{1,0:T(8,128)(2,1)} %x_ref.1, ...), custom_call_target="tpu_custom_call" | custom-call | tf_op jit(solution)/shard_map/backward/pallas_call | solution.py:423
  152.8 3.2 %write_dw.1 = (bf16[2048,640]{1,0:T(8,128)(2,1)}, bf16[2048,640]{1,0:T(8,128)(2,1)}, bf16[640,2048]{1,0:T(8,128)(2,1)}, f32[8,128]{1,0:T(8,128)S(1)}) custom-call(bf16[2048,640]{1,0:T(8,128)(2,1)S(1)} %get-tuple-element.17.dwg, bf16[2048,640]{1,0:T(8,128)(2,1)S(1)} %get-tuple-element.18.dwu, bf16[640,2048]{1,0:T(8,128)(2,1)S(1)} %get-tuple-element.19.dwd), custom_call_target="tpu_custom_call" | custom-call | tf_op jit(solution)/shard_map/write_dw/pallas_call | solution.py:447
  156.0 50.0 %exchange.1.got = bf16[4,256,2048]{2,1,0:T(8,128)(2,1)S(1)} custom-call(f32[4,256,2048]{2,1,0:T(8,128)S(1)} %get-tuple-element.14.sums, bf16[4,256,2048]{2,1,0:T(8,128)(2,1)S(1)} %get-tuple-element.15.rs_out, bf16[2,2,256,2048]{3,2,1,0:T(8,128)(2,1)} %get-tuple-element.16.rs_in, f32[8,128]{1,0:T(8,128)S(1)} %get-tuple-element.20.done), custom_call_target="tpu_custom_call" | custom-call | tf_op jit(solution)/shard_map/exchange/pallas_call | solution.py:456
  206.0 1.3 write_dx.1

commit v12 on v11

--- a/solution.py
+++ b/solution.py
@@ -159,9 +159,8 @@
     load_gates(0)
     pltpu.make_async_copy(wg_ref, wgu.at[:, pl.ds(0, F)], w_sem.at[1]).start()
     pltpu.make_async_copy(wu_ref, wgu.at[:, pl.ds(F, F)], w_sem.at[1]).start()
-    load_mine(dy_ref, dy_all, 0)
     from_partner(dy_all, dy_s, dyp_r, 0)
-    load_theirs(dy_all, 0)
+    load(dy_ref, dy_all, 0)
     acc[...] = jnp.zeros_like(acc)
     pltpu.make_async_copy(wd_ref, wd, w_sem.at[0]).wait()
     pltpu.make_async_copy(wgu, wgu, w_sem.at[1]).wait()

time: 208 us -> 208 us (level)
  no operation moved by 1% of the time
where the time goes in v12:
time: 208 us; the launch traced here: 207 us
  Pallas kernels  207 us (100%)
    pallas_call x1, Pallas kernels, local(): pl.pallas_call(kernel, out_shape=[pltpu.VMEM((4, H, D), F32), pltpu.VMEM(...  152 us
    pallas_call x1, Pallas kernels, local(): pl.pallas_call(exchange, out_shape=pltpu.VMEM((4, H, D), BF16), in_specs=...  50 us

profile of v12, /device:TPU:1, one launch (start us, length us, event | category | flops | bytes accessed | tf_op | source)
XLA Modules:
  0.0 207.4 jit_solution(2271603469118835774)
XLA Ops:
  0.6 152.1 %backward.1 = (f32[4,256,2048]{2,1,0:T(8,128)S(1)}, bf16[4,256,2048]{2,1,0:T(8,128)(2,1)S(1)}, bf16[2048,640]{1,0:T(8,128)(2,1)S(1)}, bf16[2048,640]{1,0:T(8,128...) custom-call(bf16[512,2048]{1,0:T(8,128)(2,1)} %x_ref.1, ...), custom_call_target="tpu_custom_call" | custom-call | tf_op jit(solution)/shard_map/backward/pallas_call | solution.py:422
  152.8 3.2 %write_dw.1 = (bf16[2048,640]{1,0:T(8,128)(2,1)}, bf16[2048,640]{1,0:T(8,128)(2,1)}, bf16[640,2048]{1,0:T(8,128)(2,1)}, f32[8,128]{1,0:T(8,128)S(1)}) custom-call(bf16[2048,640]{1,0:T(8,128)(2,1)S(1)} %get-tuple-element.17.dwg, bf16[2048,640]{1,0:T(8,128)(2,1)S(1)} %get-tuple-element.18.dwu, bf16[640,2048]{1,0:T(8,128)(2,1)S(1)} %get-tuple-element.19.dwd), custom_call_target="tpu_custom_call" | custom-call | tf_op jit(solution)/shard_map/write_dw/pallas_call | solution.py:446
  156.0 50.0 %exchange.1.got = bf16[4,256,2048]{2,1,0:T(8,128)(2,1)S(1)} custom-call(f32[4,256,2048]{2,1,0:T(8,128)S(1)} %get-tuple-element.14.sums, bf16[4,256,2048]{2,1,0:T(8,128)(2,1)S(1)} %get-tuple-element.15.rs_out, bf16[2,2,256,2048]{3,2,1,0:T(8,128)(2,1)} %get-tuple-element.16.rs_in, f32[8,128]{1,0:T(8,128)S(1)} %get-tuple-element.20.done), custom_call_target="tpu_custom_call" | custom-call | tf_op jit(solution)/shard_map/exchange/pallas_call | solution.py:455
  206.0 1.3 write_dx.1
